TPU v7x, 128 devices: a whole 4x4x4 slice. The times are simulated.
128 devices in a mesh: node: 4 (over y), torus: 32 (over z, x, core).
Axes of the slice: x: 4, y: 4, z: 4, core: 2. Of those that a mesh axis runs over, the one named last changes fastest.
Arguments:
- tokens: bfloat16 [16384, 7168], P(('node', 'torus')), may hold values from -6 to 6
- expert_ids: int32 [16384, 8], P(('node', 'torus')), may hold values from 0 to 383, as said below
- route_weight: bfloat16 [16384, 8], P(('node', 'torus')), may hold values from 0.19921875 to 2.5
- w_gate: bfloat16 [64, 7168, 1024], P('torus', None, 'node'), may hold values from -0.0625 to 0.0625
- w_up: bfloat16 [64, 7168, 1024], P('torus', None, 'node'), may hold values from -0.0625 to 0.0625
- w_down: bfloat16 [64, 1024, 7168], P('torus', 'node'), may hold values from -0.1875 to 0.1875
Outputs:
- moe_out: bfloat16 [16384, 7168], P(('node', 'torus'))
Inputs may be any that keep to these rules, and one draw needn't show every extreme that they name: `expert_ids`: each row names 8 different experts. Counting an expert e below 64 as one of group e // 2, at most 4 of the 128 rows of one device (aligned blocks of rows, in order) name an expert of any one group, and in every draw some group is named by exactly 4 rows of every device.
All inputs are finite; a program needn't handle non-finite values.
Results may differ from a plain program's by a relative error of at most 0.0095.
Values may be sent and summed in bfloat16 or wider, within the bound.
A program may use at most 128 MiB of HBM per device.

v0:
```python
import functools

import jax
import jax.numpy as jnp
from jax import lax
from jax.experimental import pallas as pl
from jax.experimental.pallas import tpu as pltpu
from jax.sharding import PartitionSpec as P

EXP_DEV = 2
CAP = 4
QBLOCK = 128
LANES = 128
CHUNK = 1024
MESH = pl.DeviceIdType.MESH
F32 = jnp.float32
BF16 = jnp.bfloat16

TOK, PS, PR, YRS, YRR, YLS, YLR, XRS, XRR, XLS, XLR = range(11)
ORS, ORR, OLS, OLR, NRS, NRR, NLS, NLR, RS, RR, WT, OUT = range(11, 23)
N_SEMS = 23


def dot(a, b):
    return jnp.dot(a, b, preferred_element_type=F32)


def layer(
    nodes,
    groups,
    tok_hbm,
    ids_ref,
    rw_ref,
    wg_hbm,
    wu_hbm,
    wd_hbm,
    out_hbm,
    tok,
    wg,
    wu,
    wd,
    sbuf,
    rbuf,
    xbuf,
    wsb,
    wrb,
    wx,
    acc,
    hid,
    opr,
    opl,
    opr_in,
    opl_in,
    nbr,
    nbl,
    nbr_in,
    nbl_in,
    rsb,
    rrb,
    outv,
    place_ref,
    place_t_ref,
    sems,
):
    chunks, rows_tok, width = tok.shape
    slots = groups * CAP
    half = slots // 2
    ff = wg.shape[2]
    me_n = lax.axis_index("node")
    me_t = lax.axis_index("torus")
    right = (lax.rem(me_n + 1, nodes), me_t)
    left = (lax.rem(me_n + nodes - 1, nodes), me_t)

    def plane_peer(r):
        return (me_n, lax.rem(me_t + r, groups))

    def remote(src, dst, send, recv, device):
        return pltpu.make_async_remote_copy(
            src_ref=src,
            dst_ref=dst,
            send_sem=send,
            recv_sem=recv,
            device_id=device,
            device_id_type=MESH,
        )

    def spread(src, dst, send, recv):
        def one(r, carry):
            remote(src.at[r], dst.at[groups - r], send, recv, plane_peer(r)).start()
            return carry

        lax.fori_loop(1, groups, one, 0)

    def spread_desc(src, dst, send, recv):
        return remote(
            src.at[pl.ds(1, groups - 1)], dst.at[pl.ds(1, groups - 1)], send, recv, plane_peer(1)
        )

    barrier = pltpu.get_barrier_semaphore()

    def hello(r, carry):
        pl.semaphore_signal(barrier, inc=1, device_id=plane_peer(r), device_id_type=MESH)
        return carry

    lax.fori_loop(1, groups, hello, 0)
    pl.semaphore_signal(barrier, inc=1, device_id=right, device_id_type=MESH)
    pl.semaphore_signal(barrier, inc=1, device_id=left, device_id_type=MESH)

    def tok_copy(c):
        return pltpu.make_async_copy(
            tok_hbm.at[:, pl.ds(pl.multiple_of(c * width, width), width)],
            tok.at[c],
            sems.at[TOK, c],
        )

    def wd_copy(c):
        return pltpu.make_async_copy(
            wd_hbm.at[:, pl.ds(pl.multiple_of(c * width, width), width)],
            wd.at[c],
            sems.at[WT, c],
        )

    wg_copy = pltpu.make_async_copy(wg_hbm, wg, sems.at[TOK, chunks])
    wu_copy = pltpu.make_async_copy(wu_hbm, wu, sems.at[WT, chunks])
    for c in range(chunks):
        tok_copy(c).start()
    wg_copy.start()
    wu_copy.start()
    for c in range(chunks):
        wd_copy(c).start()

    slot = lax.broadcasted_iota(jnp.int32, (rows_tok, slots), 1)
    row = lax.broadcasted_iota(jnp.int32, (rows_tok, slots), 0)
    group = lax.rem(me_t + (slot >> 2), groups)
    ids = ids_ref[...]
    weights = rw_ref[...].astype(F32)
    member = jnp.zeros((rows_tok, slots), F32)
    weight_a = jnp.zeros((rows_tok, slots), F32)
    weight_b = jnp.zeros((rows_tok, slots), F32)
    for k in range(ids.shape[1]):
        one = jnp.broadcast_to(ids[:, k : k + 1], (rows_tok, slots))
        gain = jnp.broadcast_to(weights[:, k : k + 1], (rows_tok, slots))
        is_a = one == 2 * group
        is_b = one == 2 * group + 1
        weight_a = jnp.where(is_a, gain, weight_a)
        weight_b = jnp.where(is_b, gain, weight_b)
        member = jnp.where(is_a | is_b, jnp.float32(1.0), member)
    before = (
        lax.broadcasted_iota(jnp.int32, (rows_tok, rows_tok), 1)
        < lax.broadcasted_iota(jnp.int32, (rows_tok, rows_tok), 0)
    )
    before = jnp.where(before, jnp.float32(1.0), jnp.float32(0.0)).astype(BF16)
    index = dot(before, member.astype(BF16))
    here = index == (slot & (CAP - 1)).astype(F32)
    place_t = jnp.where(here, member, jnp.float32(0.0))
    place_t_ref[...] = place_t.astype(BF16)
    place_ref[...] = jnp.transpose(place_t).astype(BF16)
    lane = lax.broadcasted_iota(jnp.int32, (rows_tok, LANES), 1)
    low = jnp.where(lane < LANES // 2, jnp.float32(1.0), jnp.float32(0.0))
    spread_w = dot(jnp.transpose(place_t * weight_a).astype(BF16), low.astype(BF16)) + dot(
        jnp.transpose(place_t * weight_b).astype(BF16), (1.0 - low).astype(BF16)
    )
    wsb[...] = spread_w.reshape(groups, CAP, LANES).astype(BF16)

    def prepare(c):
        tok_copy(c).wait()
        parts = []
        for b in range(width // QBLOCK):
            x = tok[c, :, b * QBLOCK : (b + 1) * QBLOCK].astype(F32)
            top = jnp.max(jnp.abs(x), axis=1, keepdims=True)
            scale = ((top + 1e-06) * (1.0 / 448.0)).astype(BF16).astype(F32)
            scale = jnp.broadcast_to(scale, x.shape)
            quantized = (x / scale).astype(BF16)
            parts.append((quantized.astype(F32) * scale).astype(BF16))
        restored = jnp.concatenate(parts, axis=1)
        rows = dot(place_ref[...], restored)
        sbuf[c] = rows.reshape(groups, CAP, width).astype(BF16)

    def send_plane(c):
        spread(sbuf.at[c], rbuf.at[c], sems.at[PS, c], sems.at[PR, c])

    def y_send(block, c):
        return (
            remote(block.at[0], block.at[3], sems.at[YRS, c], sems.at[YRR, c], right),
            remote(block.at[0], block.at[1], sems.at[YLS, c], sems.at[YLR, c], left),
        )

    def y_relay(block, c):
        low_rows, high_rows = pl.ds(0, half), pl.ds(half, half)
        return (
            remote(
                block.at[3, low_rows], block.at[2, low_rows], sems.at[XRS, c], sems.at[XRR, c], right
            ),
            remote(
                block.at[1, high_rows], block.at[2, high_rows], sems.at[XLS, c], sems.at[XLR, c], left
            ),
        )

    def arrive(send, arrived, block, c):
        spread_desc(send, arrived, sems.at[PS, c], sems.at[PR, c]).wait_recv()
        arrived[0] = send[0]
        rows = arrived[...].astype(F32).reshape(slots, arrived.shape[2])
        block[0] = rows.astype(BF16)
        for copy in y_send(block, c):
            copy.start()

    def pass_on(block, c):
        for copy in y_send(block, c):
            copy.wait_recv()
        for copy in y_relay(block, c):
            copy.start()

    def multiply(c):
        for copy in y_relay(xbuf.at[c], c):
            copy.wait_recv()
        x = xbuf[c].reshape(nodes * slots, width)
        at = pl.ds(pl.multiple_of(c * width, width), width)
        for e in range(EXP_DEV):
            acc[2 * e] += dot(x, wg[e, at, :])
            acc[2 * e + 1] += dot(x, wu[e, at, :])

    acc[...] = jnp.zeros_like(acc)
    prepare(0)
    pl.semaphore_wait(barrier, groups + 1)
    send_plane(0)
    spread(wsb, wrb, sems.at[PS, chunks], sems.at[PR, chunks])

    def dispatch(s, carry):
        @pl.when((s >= 1) & (s < chunks))
        def _():
            prepare(s)
            send_plane(s)

        @pl.when((s >= 2) & (s < chunks + 2))
        def _():
            arrive(sbuf.at[s - 2], rbuf.at[s - 2], xbuf.at[s - 2], s - 2)

        @pl.when((s >= 4) & (s < chunks + 4))
        def _():
            pass_on(xbuf.at[s - 4], s - 4)

        @pl.when(s == 4)
        def _():
            wg_copy.wait()
            wu_copy.wait()
            arrive(wsb, wrb, wx, chunks)

        @pl.when(s == 6)
        def _():
            pass_on(wx, chunks)

        @pl.when(s >= 5)
        def _():
            multiply(s - 5)

        return carry

    lax.fori_loop(0, chunks + 5, dispatch, 0)
    for copy in y_relay(wx, chunks):
        copy.wait_recv()

    w_all = wx[...].reshape(nodes * slots, LANES).astype(F32)
    for e in range(EXP_DEV):
        gate = acc[2 * e]
        gain = jnp.broadcast_to(w_all[:, e * (LANES // 2) : e * (LANES // 2) + 1], gate.shape)
        value = gate / (1.0 + jnp.exp(-gate)) * acc[2 * e + 1] * gain
        hid[:, e * ff : (e + 1) * ff] = value.astype(BF16)

    def opposite(c):
        return (
            remote(opr.at[c], opr_in.at[c], sems.at[ORS, c], sems.at[ORR, c], right),
            remote(opl.at[c], opl_in.at[c], sems.at[OLS, c], sems.at[OLR, c], left),
        )

    def neighbour(c):
        return (
            remote(nbr.at[c], nbr_in.at[c], sems.at[NRS, c], sems.at[NRR, c], right),
            remote(nbl.at[c], nbl_in.at[c], sems.at[NLS, c], sems.at[NLR, c], left),
        )

    def start_opposite(c):
        wd_copy(c).wait()
        part = dot(hid[2 * slots : 3 * slots, :], wd[c])
        opr[c] = part[:half].astype(BF16)
        opl[c] = part[half:].astype(BF16)
        for copy in opposite(c):
            copy.start()

    def start_neighbour(c):
        for copy in opposite(c):
            copy.wait_recv()
        part = dot(hid[slots : 2 * slots, :], wd[c])
        nbr[c, :half] = (part[:half] + opr_in[c].astype(F32)).astype(BF16)
        nbr[c, half:] = part[half:].astype(BF16)
        part = dot(hid[3 * slots :, :], wd[c])
        nbl[c, :half] = part[:half].astype(BF16)
        nbl[c, half:] = (part[half:] + opl_in[c].astype(F32)).astype(BF16)
        for copy in neighbour(c):
            copy.start()

    def finish(c):
        for copy in neighbour(c):
            copy.wait_recv()
        part = dot(hid[:slots, :], wd[c])
        part = part + nbr_in[c].astype(F32) + nbl_in[c].astype(F32)
        rsb[c] = part.reshape(groups, CAP, width).astype(BF16)
        spread(rsb.at[c], rrb.at[c], sems.at[RS, c], sems.at[RR, c])

    def out_copy(c):
        return pltpu.make_async_copy(
            outv.at[c],
            out_hbm.at[:, pl.ds(pl.multiple_of(c * width, width), width)],
            sems.at[OUT, c],
        )

    def collect(c):
        spread_desc(rsb.at[c], rrb.at[c], sems.at[RS, c], sems.at[RR, c]).wait_recv()
        rrb[c, 0] = rsb[c, 0]
        back = rrb[c].astype(F32).reshape(slots, width).astype(BF16)
        outv[c] = dot(place_t_ref[...], back).astype(BF16)
        out_copy(c).start()

    def give_back(s, carry):
        @pl.when(s < chunks)
        def _():
            start_opposite(s)

        @pl.when((s >= 2) & (s < chunks + 2))
        def _():
            start_neighbour(s - 2)

        @pl.when((s >= 4) & (s < chunks + 4))
        def _():
            finish(s - 4)

        @pl.when(s >= 6)
        def _():
            collect(s - 6)

        return carry

    lax.fori_loop(0, chunks + 6, give_back, 0)

    def drain(c, carry):
        spread_desc(sbuf.at[c], rbuf.at[c], sems.at[PS, c], sems.at[PR, c]).wait_send()
        spread_desc(rsb.at[c], rrb.at[c], sems.at[RS, c], sems.at[RR, c]).wait_send()
        for copy in y_send(xbuf.at[c], c) + y_relay(xbuf.at[c], c) + opposite(c) + neighbour(c):
            copy.wait_send()
        out_copy(c).wait()
        return carry

    lax.fori_loop(0, chunks, drain, 0)
    spread_desc(wsb, wrb, sems.at[PS, chunks], sems.at[PR, chunks]).wait_send()
    for copy in y_send(wx, chunks) + y_relay(wx, chunks):
        copy.wait_send()


def solution(mesh):
    nodes, groups = mesh.shape["node"], mesh.shape["torus"]

    def shards(tokens, expert_ids, route_weight, w_gate, w_up, w_down):
        rows_tok, depth = tokens.shape
        ff = w_gate.shape[2]
        width = min(CHUNK, depth)
        chunks = depth // width
        slots = groups * CAP
        half = slots // 2
        anywhere = pl.BlockSpec(memory_space=pl.ANY)
        inside = pl.BlockSpec(memory_space=pltpu.VMEM)
        block = pltpu.VMEM((chunks, groups, CAP, width), BF16)
        halves = pltpu.VMEM((chunks, half, width), BF16)
        whole = pltpu.VMEM((chunks, slots, width), BF16)
        return pl.pallas_call(
            functools.partial(layer, nodes, groups),
            out_shape=jax.ShapeDtypeStruct((rows_tok, depth), BF16),
            in_specs=[anywhere, inside, inside, anywhere, anywhere, anywhere],
            out_specs=anywhere,
            scratch_shapes=[
                pltpu.VMEM((chunks, rows_tok, width), BF16),
                pltpu.VMEM(w_gate.shape, BF16),
                pltpu.VMEM(w_up.shape, BF16),
                pltpu.VMEM((chunks, EXP_DEV * ff, width), BF16),
                block,
                block,
                pltpu.VMEM((chunks, nodes, slots, width), BF16),
                pltpu.VMEM((groups, CAP, LANES), BF16),
                pltpu.VMEM((groups, CAP, LANES), BF16),
                pltpu.VMEM((nodes, slots, LANES), BF16),
                pltpu.VMEM((2 * EXP_DEV, nodes * slots, ff), F32),
                pltpu.VMEM((nodes * slots, EXP_DEV * ff), BF16),
                halves,
                halves,
                halves,
                halves,
                whole,
                whole,
                whole,
                whole,
                block,
                block,
                pltpu.VMEM((chunks, rows_tok, width), BF16),
                pltpu.VMEM((slots, rows_tok), BF16),
                pltpu.VMEM((rows_tok, slots), BF16),
                pltpu.SemaphoreType.DMA((N_SEMS, chunks + 1)),
            ],
            compiler_params=pltpu.CompilerParams(
                collective_id=0, has_side_effects=True, vmem_limit_bytes=67043328
            ),
        )(
            tokens,
            expert_ids,
            route_weight,
            w_gate,
            w_up,
            w_down.reshape(EXP_DEV * ff, depth),
        )

    placed = (
        P(("node", "torus"), None),
        P(("node", "torus"), None),
        P(("node", "torus"), None),
        P("torus", None, "node"),
        P("torus", None, "node"),
        P("torus", "node", None),
    )
    return jax.shard_map(
        shards, mesh=mesh, in_specs=placed, out_specs=P(("node", "torus"), None), check_vma=False
    )
```

profile of v0, /device:TPU:1, one launch (start us, length us, event | category | flops | bytes accessed | tf_op | source)
XLA Modules:
  0.0 156.2 jit_solution(4919121459793631918)
XLA Ops:
  0.0 1.4 copy.8.rw_ref
  1.4 1.4 copy.7.ids_ref
  2.8 150.6 %shard_map.64 = bf16[128,7168]{1,0:T(8,128)(2,1)} custom-call(bf16[128,7168]{1,0:T(8,128)(2,1)} %tok_hbm.1, s32[128,8]{1,0:T(8,128)} %copy.7.ids_ref, bf16[128,8]{1,0:T(8,128)(2,1)} %copy.8.rw_ref, bf16[2,7168,256]{2,1,0:T(8,128)(2,1)} %wg_hbm.1, bf16[2,7168,256]{2,1,0:T(8,128)(2,1)} %wu_hbm.1, bf16[512,7168]{1,0:T(8,128)(2,1)} %bitcast.1), custom_call_target="tpu_custom_call" | custom-call | tf_op jit(solution)/shard_map/pallas_call | solution.py:373
  153.4 2.8 %copy.10 = bf16[128,7168]{1,0:T(8,128)(2,1)} copy(bf16[128,7168]{1,0:T(8,128)(2,1)} %shard_map.64) | data formatting | bytes 3670016
where the time goes:
time: 157 us; the launch traced here: 156 us
  Pallas kernels  151 us (96%)
  local copies, waits for them, and re-layouts  5.64 us (4%)
    pallas_call x1, Pallas kernels, shards(): pl.pallas_call(functools.partial(layer, nodes, groups), out_shape=jax.Sha...  151 us
    unnamed x3, local copies, waits for them, and re-layouts  5.64 us

commit v1 on v0

v1 whole, which is shorter than its diff:
```python
import functools

import jax
import jax.numpy as jnp
from jax import lax
from jax.experimental import pallas as pl
from jax.experimental.pallas import tpu as pltpu
from jax.sharding import PartitionSpec as P

EXP_DEV = 2
CAP = 4
QBLOCK = 128
LANES = 128
CHUNK = 1024
BATCHES = 2
MESH = pl.DeviceIdType.MESH
F32 = jnp.float32
BF16 = jnp.bfloat16

TOK, PS, PR, YRS, YRR, YLS, YLR, XRS, XRR, XLS, XLR = range(11)
ORS, ORR, OLS, OLR, NRS, NRR, NLS, NLR, RS, RR, WT, OUT = range(11, 23)
N_SEMS = 23


def dot(a, b):
    return jnp.dot(a, b, preferred_element_type=F32)


def layer(
    nodes,
    groups,
    tok_hbm,
    ids_ref,
    rw_ref,
    wg_hbm,
    wu_hbm,
    wd_hbm,
    out_hbm,
    tok,
    wg,
    wu,
    wd,
    sbuf,
    rbuf,
    xbuf,
    wsb,
    wrb,
    wx,
    acc,
    hid,
    opr,
    opl,
    opr_in,
    opl_in,
    nbr,
    nbl,
    nbr_in,
    nbl_in,
    rsb,
    rrb,
    outv,
    place_ref,
    place_t_ref,
    sems,
):
    chunks, rows_tok, width = tok.shape
    steps = BATCHES * chunks
    some = groups // BATCHES
    slots = groups * CAP
    rows = some * CAP
    half = rows // 2
    ff = wg.shape[2]
    me_n = lax.axis_index("node")
    me_t = lax.axis_index("torus")
    right = (lax.rem(me_n + 1, nodes), me_t)
    left = (lax.rem(me_n + nodes - 1, nodes), me_t)
    OWN, RIGHT, LEFT, FAR = range(4)

    def plane_peer(r):
        return (me_n, lax.rem(me_t + r, groups))

    def remote(src, dst, send, recv, device):
        return pltpu.make_async_remote_copy(
            src_ref=src,
            dst_ref=dst,
            send_sem=send,
            recv_sem=recv,
            device_id=device,
            device_id_type=MESH,
        )

    def spread(src, dst, send, recv, batch):
        def one(j, carry):
            peer = plane_peer(BATCHES * j + batch)
            remote(src.at[j], dst.at[some - batch - j], send, recv, peer).start()
            return carry

        lax.fori_loop(1 - batch, some, one, 0)

    def spread_desc(src, dst, send, recv, low, high):
        at = pl.ds(low, high - low)
        return remote(src.at[at], dst.at[at], send, recv, plane_peer(1))

    def spread_wait(src, dst, send, recv, batch, received):
        for b in range(BATCHES):

            @pl.when(batch == b)
            def _(b=b):
                copy = spread_desc(src, dst, send, recv, 1 - b, some)
                if received:
                    copy.wait_recv()
                else:
                    copy.wait_send()

    barrier = pltpu.get_barrier_semaphore()

    def hello(r, carry):
        pl.semaphore_signal(barrier, inc=1, device_id=plane_peer(r), device_id_type=MESH)
        return carry

    lax.fori_loop(1, groups, hello, 0)
    pl.semaphore_signal(barrier, inc=1, device_id=right, device_id_type=MESH)
    pl.semaphore_signal(barrier, inc=1, device_id=left, device_id_type=MESH)

    def tok_copy(c):
        return pltpu.make_async_copy(
            tok_hbm.at[:, pl.ds(pl.multiple_of(c * width, width), width)],
            tok.at[c],
            sems.at[TOK, c],
        )

    def wd_copy(c):
        return pltpu.make_async_copy(
            wd_hbm.at[:, pl.ds(pl.multiple_of(c * width, width), width)],
            wd.at[c],
            sems.at[WT, c],
        )

    wg_copy = pltpu.make_async_copy(wg_hbm, wg, sems.at[TOK, chunks])
    wu_copy = pltpu.make_async_copy(wu_hbm, wu, sems.at[WT, chunks])
    for c in range(chunks):
        tok_copy(c).start()
    wg_copy.start()
    wu_copy.start()
    for c in range(chunks):
        wd_copy(c).start()

    slot = lax.broadcasted_iota(jnp.int32, (slots, rows_tok), 0)
    spot = slot // CAP
    offset = BATCHES * lax.rem(spot, some) + spot // some
    group = lax.rem(me_t + offset, groups)
    ids = ids_ref[...]
    weights = rw_ref[...].astype(F32)
    member = jnp.zeros((slots, rows_tok), F32)
    weight_a = jnp.zeros((slots, rows_tok), F32)
    weight_b = jnp.zeros((slots, rows_tok), F32)
    for k in range(ids.shape[0]):
        one = jnp.broadcast_to(ids[k : k + 1, :], (slots, rows_tok))
        gain = jnp.broadcast_to(weights[k : k + 1, :], (slots, rows_tok))
        is_a = one == 2 * group
        is_b = one == 2 * group + 1
        weight_a = jnp.where(is_a, gain, weight_a)
        weight_b = jnp.where(is_b, gain, weight_b)
        member = jnp.where(is_a | is_b, jnp.float32(1.0), member)
    before = (
        lax.broadcasted_iota(jnp.int32, (rows_tok, rows_tok), 0)
        < lax.broadcasted_iota(jnp.int32, (rows_tok, rows_tok), 1)
    )
    before = jnp.where(before, jnp.float32(1.0), jnp.float32(0.0)).astype(BF16)
    index = dot(member.astype(BF16), before)
    here = index == lax.rem(slot, CAP).astype(F32)
    place = jnp.where(here, member, jnp.float32(0.0))
    place_ref[...] = place.astype(BF16)
    place_t_ref[...] = jnp.transpose(place).astype(BF16)
    lane = lax.broadcasted_iota(jnp.int32, (rows_tok, LANES), 1)
    low = jnp.where(lane < LANES // 2, jnp.float32(1.0), jnp.float32(0.0))
    spread_w = dot((place * weight_a).astype(BF16), low.astype(BF16)) + dot(
        (place * weight_b).astype(BF16), (1.0 - low).astype(BF16)
    )
    wsb[...] = spread_w.reshape(groups, CAP, LANES).astype(BF16)

    def prepare(c):
        tok_copy(c).wait()
        parts = []
        for b in range(width // QBLOCK):
            x = tok[c, :, b * QBLOCK : (b + 1) * QBLOCK].astype(F32)
            top = jnp.max(jnp.abs(x), axis=1, keepdims=True)
            scale = ((top + 1e-06) * (1.0 / 448.0)).astype(BF16).astype(F32)
            scale = jnp.broadcast_to(scale, x.shape)
            quantized = (x / scale).astype(BF16)
            parts.append((quantized.astype(F32) * scale).astype(BF16))
        restored = jnp.concatenate(parts, axis=1)
        picked = dot(place_ref[...], restored).reshape(groups, CAP, width).astype(BF16)
        for b in range(BATCHES):
            sbuf[b * chunks + c] = picked[b * some : (b + 1) * some]

    def send_plane(u):
        spread(sbuf.at[u], rbuf.at[u], sems.at[PS, u], sems.at[PR, u], u // chunks)

    def y_send(block, u):
        return (
            remote(block.at[OWN], block.at[LEFT], sems.at[YRS, u], sems.at[YRR, u], right),
            remote(block.at[OWN], block.at[RIGHT], sems.at[YLS, u], sems.at[YLR, u], left),
        )

    def y_relay(block, u):
        middle = block.shape[1] // 2
        low, high = pl.ds(0, middle), pl.ds(middle, middle)
        return (
            remote(block.at[LEFT, low], block.at[FAR, low], sems.at[XRS, u], sems.at[XRR, u], right),
            remote(block.at[RIGHT, high], block.at[FAR, high], sems.at[XLS, u], sems.at[XLR, u], left),
        )

    def flat(ref_value):
        count, cap, lanes = ref_value.shape
        return ref_value.astype(F32).reshape(count * cap, lanes).astype(BF16)

    def arrive(u):
        batch = u // chunks
        spread_wait(sbuf.at[u], rbuf.at[u], sems.at[PS, u], sems.at[PR, u], batch, True)

        @pl.when(batch == 0)
        def _():
            rbuf[u, 0] = sbuf[u, 0]

        xbuf[u, OWN] = flat(rbuf[u])
        for copy in y_send(xbuf.at[u], u):
            copy.start()

    def pass_on(block, u):
        for copy in y_send(block, u):
            copy.wait_recv()
        for copy in y_relay(block, u):
            copy.start()

    def multiply(u):
        for copy in y_relay(xbuf.at[u], u):
            copy.wait_recv()
        batch = u // chunks
        x = xbuf[u].reshape(nodes * rows, width)
        at = pl.ds(pl.multiple_of((u - batch * chunks) * width, width), width)
        for e in range(EXP_DEV):
            acc[batch, 2 * e] += dot(x, wg[e, at, :])
            acc[batch, 2 * e + 1] += dot(x, wu[e, at, :])

    def activate(batch):
        w_all = wx[:, pl.ds(pl.multiple_of(batch * rows, rows), rows), :]
        w_all = w_all.astype(F32).reshape(nodes * rows, LANES)
        for e in range(EXP_DEV):
            gate = acc[batch, 2 * e]
            gain = jnp.broadcast_to(w_all[:, e * (LANES // 2) : e * (LANES // 2) + 1], gate.shape)
            value = gate / (1.0 + jnp.exp(-gate)) * acc[batch, 2 * e + 1] * gain
            hid[batch, :, e * ff : (e + 1) * ff] = value.astype(BF16)

    def opposite(u):
        return (
            remote(opr.at[u], opr_in.at[u], sems.at[ORS, u], sems.at[ORR, u], right),
            remote(opl.at[u], opl_in.at[u], sems.at[OLS, u], sems.at[OLR, u], left),
        )

    def neighbour(u):
        return (
            remote(nbr.at[u], nbr_in.at[u], sems.at[NRS, u], sems.at[NRR, u], right),
            remote(nbl.at[u], nbl_in.at[u], sems.at[NLS, u], sems.at[NLR, u], left),
        )

    def project(u, first, count):
        batch = u // chunks
        return dot(hid[batch, first * rows : (first + count) * rows, :], wd[u - batch * chunks])

    def start_opposite(u):
        @pl.when(u < chunks)
        def _():
            wd_copy(u).wait()

        part = project(u, FAR, 1)
        opr[u] = part[:half].astype(BF16)
        opl[u] = part[half:].astype(BF16)
        for copy in opposite(u):
            copy.start()

    def start_neighbour(u):
        part = project(u, RIGHT, 2)
        for copy in opposite(u):
            copy.wait_recv()
        nbr[u, :half] = (part[:half] + opr_in[u].astype(F32)).astype(BF16)
        nbr[u, half:] = part[half:rows].astype(BF16)
        nbl[u, :half] = part[rows : rows + half].astype(BF16)
        nbl[u, half:] = (part[rows + half :] + opl_in[u].astype(F32)).astype(BF16)
        for copy in neighbour(u):
            copy.start()

    def finish(u):
        part = project(u, OWN, 1)
        for copy in neighbour(u):
            copy.wait_recv()
        part = part + nbr_in[u].astype(F32) + nbl_in[u].astype(F32)
        rsb[u] = part.reshape(some, CAP, width).astype(BF16)
        spread(rsb.at[u], rrb.at[u], sems.at[RS, u], sems.at[RR, u], u // chunks)

    def out_copy(c):
        return pltpu.make_async_copy(
            outv.at[c],
            out_hbm.at[:, pl.ds(pl.multiple_of(c * width, width), width)],
            sems.at[OUT, c],
        )

    def collect(c):
        total = jnp.zeros((rows_tok, width), F32)
        for b in range(BATCHES):
            u = b * chunks + c
            spread_desc(
                rsb.at[u], rrb.at[u], sems.at[RS, u], sems.at[RR, u], 1 - b, some
            ).wait_recv()
            if b == 0:
                rrb[u, 0] = rsb[u, 0]
            total += dot(place_t_ref[:, b * rows : (b + 1) * rows], flat(rrb[u]))
        outv[c] = total.astype(BF16)
        out_copy(c).start()

    acc[...] = jnp.zeros_like(acc)
    prepare(0)
    pl.semaphore_wait(barrier, groups + 1)
    send_plane(0)
    for b in range(BATCHES):
        at = pl.ds(b * some, some)
        spread(wsb.at[at], wrb.at[at], sems.at[PS, steps], sems.at[PR, steps], b)

    lag_y, lag_x, lag_m = 2, 4, 5
    lag_o = steps + 1
    lag_n, lag_f, lag_c = lag_o + 2, lag_o + 4, lag_o + 6

    def stage(s, lag, first, last, work):
        @pl.when((s >= lag + first) & (s < lag + last))
        def _():
            work(s - lag)

    def whole(s, carry):
        stage(s, 0, 1, chunks, prepare)
        stage(s, 0, 1, steps, send_plane)
        stage(s, lag_y, 0, steps, arrive)

        @pl.when(s == 3)
        def _():
            spread_desc(wsb, wrb, sems.at[PS, steps], sems.at[PR, steps], 1, groups).wait_recv()
            wrb[0] = wsb[0]
            wx[OWN] = flat(wrb[...])
            for copy in y_send(wx, steps):
                copy.start()
            wg_copy.wait()
            wu_copy.wait()

        stage(s, lag_x, 0, steps, lambda u: pass_on(xbuf.at[u], u))

        @pl.when(s == 5)
        def _():
            pass_on(wx, steps)

        stage(s, lag_m, 0, steps, multiply)

        @pl.when(s == 7)
        def _():
            for copy in y_relay(wx, steps):
                copy.wait_recv()

        @pl.when((s == lag_m + chunks - 1) | (s == lag_m + steps - 1))
        def _():
            activate((s - lag_m) // chunks)

        stage(s, lag_o, 0, steps, start_opposite)
        stage(s, lag_n, 0, steps, start_neighbour)
        stage(s, lag_f, 0, steps, finish)
        stage(s, lag_c + steps - chunks, 0, chunks, collect)
        return carry

    lax.fori_loop(0, lag_c + steps, whole, 0)

    def drain(u, carry):
        spread_wait(sbuf.at[u], rbuf.at[u], sems.at[PS, u], sems.at[PR, u], u // chunks, False)
        spread_wait(rsb.at[u], rrb.at[u], sems.at[RS, u], sems.at[RR, u], u // chunks, False)
        for copy in y_send(xbuf.at[u], u) + y_relay(xbuf.at[u], u) + opposite(u) + neighbour(u):
            copy.wait_send()

        @pl.when(u < chunks)
        def _():
            out_copy(u).wait()

        return carry

    lax.fori_loop(0, steps, drain, 0)
    spread_desc(wsb, wrb, sems.at[PS, steps], sems.at[PR, steps], 1, groups).wait_send()
    for copy in y_send(wx, steps) + y_relay(wx, steps):
        copy.wait_send()


def solution(mesh):
    nodes, groups = mesh.shape["node"], mesh.shape["torus"]

    def shards(tokens, expert_ids, route_weight, w_gate, w_up, w_down):
        rows_tok, depth = tokens.shape
        ff = w_gate.shape[2]
        width = min(CHUNK, depth)
        chunks = depth // width
        slots = groups * CAP
        steps = BATCHES * chunks
        some = groups // BATCHES
        rows = some * CAP
        anywhere = pl.BlockSpec(memory_space=pl.ANY)
        inside = pl.BlockSpec(memory_space=pltpu.VMEM)
        block = pltpu.VMEM((steps, some, CAP, width), BF16)
        halves = pltpu.VMEM((steps, rows // 2, width), BF16)
        whole = pltpu.VMEM((steps, rows, width), BF16)
        return pl.pallas_call(
            functools.partial(layer, nodes, groups),
            out_shape=jax.ShapeDtypeStruct((rows_tok, depth), BF16),
            in_specs=[anywhere, inside, inside, anywhere, anywhere, anywhere],
            out_specs=anywhere,
            scratch_shapes=[
                pltpu.VMEM((chunks, rows_tok, width), BF16),
                pltpu.VMEM(w_gate.shape, BF16),
                pltpu.VMEM(w_up.shape, BF16),
                pltpu.VMEM((chunks, EXP_DEV * ff, width), BF16),
                block,
                block,
                pltpu.VMEM((steps, nodes, rows, width), BF16),
                pltpu.VMEM((groups, CAP, LANES), BF16),
                pltpu.VMEM((groups, CAP, LANES), BF16),
                pltpu.VMEM((nodes, slots, LANES), BF16),
                pltpu.VMEM((BATCHES, 2 * EXP_DEV, nodes * rows, ff), F32),
                pltpu.VMEM((BATCHES, nodes * rows, EXP_DEV * ff), BF16),
                halves,
                halves,
                halves,
                halves,
                whole,
                whole,
                whole,
                whole,
                block,
                block,
                pltpu.VMEM((chunks, rows_tok, width), BF16),
                pltpu.VMEM((slots, rows_tok), BF16),
                pltpu.VMEM((rows_tok, slots), BF16),
                pltpu.SemaphoreType.DMA((N_SEMS, steps + 1)),
            ],
            compiler_params=pltpu.CompilerParams(
                collective_id=0, has_side_effects=True, vmem_limit_bytes=67043328
            ),
        )(
            tokens,
            expert_ids.T,
            route_weight.T,
            w_gate,
            w_up,
            w_down.reshape(EXP_DEV * ff, depth),
        )

    placed = (
        P(("node", "torus"), None),
        P(("node", "torus"), None),
        P(("node", "torus"), None),
        P("torus", None, "node"),
        P("torus", None, "node"),
        P("torus", "node", None),
    )
    return jax.shard_map(
        shards, mesh=mesh, in_specs=placed, out_specs=P(("node", "torus"), None), check_vma=False
    )
```

time: 157 us -> 148 us (0.943)
  Pallas kernels: 151 us -> 145 us
  local copies, waits for them, and re-layouts: 5.64 us -> 2.85 us
    pallas_call x1, Pallas kernels: 151 us -> 145 us  [shards(): pl.pallas_call(functools.partial(layer, nodes, groups), out_shape=jax.Sha...]
    unnamed x3 -> x1, local copies, waits for them, and re-layouts: 5.64 us -> 2.85 us
where the time goes in v1:
time: 148 us
  Pallas kernels  145 us (98%)
  local copies, waits for them, and re-layouts  2.85 us (2%)
    pallas_call x1, Pallas kernels, shards(): pl.pallas_call(functools.partial(layer, nodes, groups), out_shape=jax.Sha...  145 us

profile of v1, /device:TPU:1, one launch (start us, length us, event | category | flops | bytes accessed | tf_op | source)
XLA Modules:
  0.0 148.2 jit_solution(13709912792923693495)
XLA Ops:
  0.0 145.4 %shard_map.64 = bf16[128,7168]{1,0:T(8,128)(2,1)} custom-call(bf16[128,7168]{1,0:T(8,128)(2,1)} %tok_hbm.1, s32[8,128]{1,0:T(8,128)} %bitcast.4, bf16[8,128]{1,0:T(8,128)(2,1)} %bitcast.5, bf16[2,7168,256]{2,1,0:T(8,128)(2,1)} %wg_hbm.1, bf16[2,7168,256]{2,1,0:T(8,128)(2,1)} %wu_hbm.1, bf16[512,7168]{1,0:T(8,128)(2,1)} %bitcast.3), custom_call_target="tpu_custom_call" | custom-call | tf_op jit(solution)/shard_map/pallas_call | solution.py:413
  145.4 2.8 %copy.8 = bf16[128,7168]{1,0:T(8,128)(2,1)} copy(bf16[128,7168]{1,0:T(8,128)(2,1)} %shard_map.64) | data formatting | bytes 3670016

commit v2 on v1

--- a/solution.py
+++ b/solution.py
@@ -58,13 +58,25 @@
     nbl_in,
     rsb,
     rrb,
+    zbuf,
+    zin,
+    wbuf,
+    win,
+    far_r,
+    far_l,
+    wnr,
+    wnl,
+    wnr_in,
+    wnl_in,
     outv,
     place_ref,
     place_t_ref,
     sems,
+    round_sems,
 ):
     chunks, rows_tok, width = tok.shape
-    steps = BATCHES * chunks
+    plain = chunks - 1
+    steps = BATCHES * plain
     some = groups // BATCHES
     slots = groups * CAP
     rows = some * CAP
@@ -112,15 +124,29 @@
                 else:
                     copy.wait_send()
 
+    across = min(4, groups // 2)
+    deep = groups // (2 * across)
+    me_core, me_x, me_z = lax.rem(me_t, 2), lax.rem(me_t // 2, across), me_t // (2 * across)
+
+    def torus_peer(dz, dx, dc):
+        z, x, core = lax.rem(me_z + dz, deep), lax.rem(me_x + dx, across), lax.rem(me_core + dc, 2)
+        return (me_n, (z * across + x) * 2 + core)
+
+    partner = [torus_peer(0, 0, 1)]
+    along_x = [torus_peer(0, 1, 0), torus_peer(0, across - 1, 0)]
+    along_z = [torus_peer(1, 0, 0), torus_peer(deep - 1, 0, 0)] if deep > 1 else []
     barrier = pltpu.get_barrier_semaphore()
-
-    def hello(r, carry):
-        pl.semaphore_signal(barrier, inc=1, device_id=plane_peer(r), device_id_type=MESH)
-        return carry
-
-    lax.fori_loop(1, groups, hello, 0)
-    pl.semaphore_signal(barrier, inc=1, device_id=right, device_id_type=MESH)
-    pl.semaphore_signal(barrier, inc=1, device_id=left, device_id_type=MESH)
+    greeted = [right, left] + partner + along_x + along_z
+    for device in greeted:
+        pl.semaphore_signal(barrier, inc=1, device_id=device, device_id_type=MESH)
+    rounds = [along_x] + [along_z] * (2 if deep > 1 else 0) + [partner]
+
+    def tell(k):
+        for device in rounds[k]:
+            pl.semaphore_signal(round_sems.at[k], inc=1, device_id=device, device_id_type=MESH)
+
+    def told(k):
+        pl.semaphore_wait(round_sems.at[k], len(rounds[k]))
 
     def tok_copy(c):
         return pltpu.make_async_copy(
@@ -191,11 +217,14 @@
             parts.append((quantized.astype(F32) * scale).astype(BF16))
         restored = jnp.concatenate(parts, axis=1)
         picked = dot(place_ref[...], restored).reshape(groups, CAP, width).astype(BF16)
-        for b in range(BATCHES):
-            sbuf[b * chunks + c] = picked[b * some : (b + 1) * some]
+        if c == 0:
+            zbuf[OWN] = picked
+        else:
+            for b in range(BATCHES):
+                sbuf[b * plain + c - 1] = picked[b * some : (b + 1) * some]
 
     def send_plane(u):
-        spread(sbuf.at[u], rbuf.at[u], sems.at[PS, u], sems.at[PR, u], u // chunks)
+        spread(sbuf.at[u], rbuf.at[u], sems.at[PS, u], sems.at[PR, u], u // plain)
 
     def y_send(block, u):
         return (
@@ -216,7 +245,7 @@
         return ref_value.astype(F32).reshape(count * cap, lanes).astype(BF16)
 
     def arrive(u):
-        batch = u // chunks
+        batch = u // plain
         spread_wait(sbuf.at[u], rbuf.at[u], sems.at[PS, u], sems.at[PR, u], batch, True)
 
         @pl.when(batch == 0)
@@ -236,12 +265,103 @@
     def multiply(u):
         for copy in y_relay(xbuf.at[u], u):
             copy.wait_recv()
-        batch = u // chunks
-        x = xbuf[u].reshape(nodes * rows, width)
-        at = pl.ds(pl.multiple_of((u - batch * chunks) * width, width), width)
+        batch = u // plain
+        add_chunk(xbuf[u].reshape(nodes * rows, width), batch, u - batch * plain + 1)
+
+    def add_chunk(x, batch, c):
+        at = pl.ds(pl.multiple_of(c * width, width), width)
         for e in range(EXP_DEV):
             acc[batch, 2 * e] += dot(x, wg[e, at, :])
             acc[batch, 2 * e + 1] += dot(x, wu[e, at, :])
+
+    def z_piece(batch):
+        return zbuf.at[:, pl.ds(batch * some, some)], steps + 1 + batch
+
+    def spread_planes(src, dst, send, recv, batch):
+        def one(j, carry):
+            peer = plane_peer(BATCHES * j + batch)
+            here, there = batch * some + j, batch * some + some - batch - j
+            remote(src.at[:, here], dst.at[:, there], send, recv, peer).start()
+            return carry
+
+        lax.fori_loop(1 - batch, some, one, 0)
+
+    def planes_desc(src, dst, send, recv, batch):
+        at = pl.ds(batch * some + 1 - batch, some - 1 + batch)
+        return remote(src.at[:, at], dst.at[:, at], send, recv, plane_peer(1))
+
+    def z_plane(batch):
+        u = steps + 1 + batch
+        return zbuf, zin, sems.at[PS, u], sems.at[PR, u], batch
+
+    def w_plane(batch):
+        u = steps + 1 + batch
+        return wbuf, win, sems.at[RS, u], sems.at[RR, u], batch
+
+    def z_out(batch):
+        for copy in y_relay(*z_piece(batch)):
+            copy.wait_recv()
+        spread_planes(*z_plane(batch))
+
+    def z_multiply(batch):
+        planes_desc(*z_plane(batch)).wait_recv()
+        if batch == 0:
+            zin[:, 0] = zbuf[:, 0]
+        x = zin[:, batch * some : (batch + 1) * some].astype(F32)
+        add_chunk(x.reshape(nodes * rows, width).astype(BF16), batch, 0)
+
+    def w_project(batch):
+        if batch == 0:
+            wd_copy(plain).wait()
+        part = dot(hid[batch], wd[plain])
+        wbuf[:, batch * some : (batch + 1) * some] = part.reshape(nodes, some, CAP, width).astype(BF16)
+        spread_planes(*w_plane(batch))
+
+    def w_far(batch):
+        u, mid = steps + 1 + batch, some // 2
+        first, second = pl.ds(batch * some, mid), pl.ds(batch * some + mid, mid)
+        return (
+            remote(win.at[FAR, first], far_r.at[batch], sems.at[ORS, u], sems.at[ORR, u], right),
+            remote(win.at[FAR, second], far_l.at[batch], sems.at[OLS, u], sems.at[OLR, u], left),
+        )
+
+    def w_near(batch):
+        u = steps + 1 + batch
+        return (
+            remote(wnr.at[batch], wnr_in.at[batch], sems.at[NRS, u], sems.at[NRR, u], right),
+            remote(wnl.at[batch], wnl_in.at[batch], sems.at[NLS, u], sems.at[NLR, u], left),
+        )
+
+    def w_opposite(batch):
+        planes_desc(*w_plane(batch)).wait_recv()
+        if batch == 0:
+            win[:, 0] = wbuf[:, 0]
+        for copy in w_far(batch):
+            copy.start()
+
+    def w_neighbour(batch):
+        low, mid, high = batch * some, batch * some + some // 2, (batch + 1) * some
+        for copy in w_far(batch):
+            copy.wait_recv()
+        wnr[batch, : some // 2] = (
+            win[RIGHT, low:mid].astype(F32) + far_r[batch].astype(F32)
+        ).astype(BF16)
+        wnr[batch, some // 2 :] = win[RIGHT, mid:high]
+        wnl[batch, : some // 2] = win[LEFT, low:mid]
+        wnl[batch, some // 2 :] = (
+            win[LEFT, mid:high].astype(F32) + far_l[batch].astype(F32)
+        ).astype(BF16)
+        for copy in w_near(batch):
+            copy.start()
+
+    def w_finish(batch):
+        for copy in w_near(batch):
+            copy.wait_recv()
+        part = win[OWN, batch * some : (batch + 1) * some].astype(F32)
+        part = part + wnr_in[batch].astype(F32) + wnl_in[batch].astype(F32)
+        return dot(
+            place_t_ref[:, batch * rows : (batch + 1) * rows], part.reshape(rows, width).astype(BF16)
+        )
 
     def activate(batch):
         w_all = wx[:, pl.ds(pl.multiple_of(batch * rows, rows), rows), :]
@@ -265,11 +385,11 @@
         )
 
     def project(u, first, count):
-        batch = u // chunks
-        return dot(hid[batch, first * rows : (first + count) * rows, :], wd[u - batch * chunks])
+        batch = u // plain
+        return dot(hid[batch, first * rows : (first + count) * rows, :], wd[u - batch * plain])
 
     def start_opposite(u):
-        @pl.when(u < chunks)
+        @pl.when(u < plain)
         def _():
             wd_copy(u).wait()
 
@@ -296,7 +416,7 @@
             copy.wait_recv()
         part = part + nbr_in[u].astype(F32) + nbl_in[u].astype(F32)
         rsb[u] = part.reshape(some, CAP, width).astype(BF16)
-        spread(rsb.at[u], rrb.at[u], sems.at[RS, u], sems.at[RR, u], u // chunks)
+        spread(rsb.at[u], rrb.at[u], sems.at[RS, u], sems.at[RR, u], u // plain)
 
     def out_copy(c):
         return pltpu.make_async_copy(
@@ -308,7 +428,7 @@
     def collect(c):
         total = jnp.zeros((rows_tok, width), F32)
         for b in range(BATCHES):
-            u = b * chunks + c
+            u = b * plain + c
             spread_desc(
                 rsb.at[u], rrb.at[u], sems.at[RS, u], sems.at[RR, u], 1 - b, some
             ).wait_recv()
@@ -318,15 +438,27 @@
         outv[c] = total.astype(BF16)
         out_copy(c).start()
 
+    prepare(0)
+    pl.semaphore_wait(barrier, len(greeted))
+    for b in range(BATCHES):
+        for copy in y_send(*z_piece(b)):
+            copy.start()
     acc[...] = jnp.zeros_like(acc)
-    prepare(0)
-    pl.semaphore_wait(barrier, groups + 1)
-    send_plane(0)
+    for c in range(1, chunks):
+        if c <= len(rounds):
+            tell(c - 1)
+        prepare(c)
+        if c <= len(rounds):
+            told(c - 1)
+    for u in range(4):
+        send_plane(u)
     for b in range(BATCHES):
         at = pl.ds(b * some, some)
         spread(wsb.at[at], wrb.at[at], sems.at[PS, steps], sems.at[PR, steps], b)
-
-    lag_y, lag_x, lag_m = 2, 4, 5
+    for b in range(BATCHES):
+        pass_on(*z_piece(b))
+
+    lag_y, lag_x, lag_m = 0, 2, 4
     lag_o = steps + 1
     lag_n, lag_f, lag_c = lag_o + 2, lag_o + 4, lag_o + 6
 
@@ -335,49 +467,69 @@
         def _():
             work(s - lag)
 
+    def at_step(s, step, work, *args):
+        @pl.when(s == step)
+        def _():
+            work(*args)
+
+    def share_weights():
+        spread_desc(wsb, wrb, sems.at[PS, steps], sems.at[PR, steps], 1, groups).wait_recv()
+        wrb[0] = wsb[0]
+        wx[OWN] = flat(wrb[...])
+        for copy in y_send(wx, steps):
+            copy.start()
+
+    def have_gate_up():
+        wg_copy.wait()
+        wu_copy.wait()
+
+    def have_weights():
+        for copy in y_relay(wx, steps):
+            copy.wait_recv()
+
+    def turn(batch):
+        z_multiply(batch)
+        activate(batch)
+        w_project(batch)
+
+    def w_last():
+        total = w_finish(0) + w_finish(1)
+        outv[plain] = total.astype(BF16)
+        out_copy(plain).start()
+
+    def send_two(k):
+        send_plane(4 + 2 * k)
+        send_plane(5 + 2 * k)
+
     def whole(s, carry):
-        stage(s, 0, 1, chunks, prepare)
-        stage(s, 0, 1, steps, send_plane)
+        stage(s, 0, 0, (steps - 4) // 2, send_two)
         stage(s, lag_y, 0, steps, arrive)
-
-        @pl.when(s == 3)
-        def _():
-            spread_desc(wsb, wrb, sems.at[PS, steps], sems.at[PR, steps], 1, groups).wait_recv()
-            wrb[0] = wsb[0]
-            wx[OWN] = flat(wrb[...])
-            for copy in y_send(wx, steps):
-                copy.start()
-            wg_copy.wait()
-            wu_copy.wait()
-
+        at_step(s, 1, share_weights)
+        at_step(s, 3, have_gate_up)
         stage(s, lag_x, 0, steps, lambda u: pass_on(xbuf.at[u], u))
-
-        @pl.when(s == 5)
-        def _():
-            pass_on(wx, steps)
-
+        at_step(s, 3, pass_on, wx, steps)
+        at_step(s, 4, z_out, 0)
+        at_step(s, 5, z_out, 1)
         stage(s, lag_m, 0, steps, multiply)
-
-        @pl.when(s == 7)
-        def _():
-            for copy in y_relay(wx, steps):
-                copy.wait_recv()
-
-        @pl.when((s == lag_m + chunks - 1) | (s == lag_m + steps - 1))
-        def _():
-            activate((s - lag_m) // chunks)
-
+        at_step(s, 6, have_weights)
+        at_step(s, steps, turn, 0)
+        at_step(s, lag_m + steps - 1, turn, 1)
         stage(s, lag_o, 0, steps, start_opposite)
+        at_step(s, lag_o + steps, w_opposite, 0)
+        at_step(s, lag_o + steps + 1, w_opposite, 1)
         stage(s, lag_n, 0, steps, start_neighbour)
+        at_step(s, lag_n + steps, w_neighbour, 0)
+        at_step(s, lag_n + steps + 1, w_neighbour, 1)
         stage(s, lag_f, 0, steps, finish)
-        stage(s, lag_c + steps - chunks, 0, chunks, collect)
+        stage(s, lag_c + steps - plain, 0, plain, collect)
+        at_step(s, lag_f + steps + 1, w_last)
         return carry
 
-    lax.fori_loop(0, lag_c + steps, whole, 0)
+    lax.fori_loop(0, lag_f + steps + 2, whole, 0)
 
     def drain(u, carry):
-        spread_wait(sbuf.at[u], rbuf.at[u], sems.at[PS, u], sems.at[PR, u], u // chunks, False)
-        spread_wait(rsb.at[u], rrb.at[u], sems.at[RS, u], sems.at[RR, u], u // chunks, False)
+        spread_wait(sbuf.at[u], rbuf.at[u], sems.at[PS, u], sems.at[PR, u], u // plain, False)
+        spread_wait(rsb.at[u], rrb.at[u], sems.at[RS, u], sems.at[RR, u], u // plain, False)
         for copy in y_send(xbuf.at[u], u) + y_relay(xbuf.at[u], u) + opposite(u) + neighbour(u):
             copy.wait_send()
 
@@ -391,6 +543,11 @@
     spread_desc(wsb, wrb, sems.at[PS, steps], sems.at[PR, steps], 1, groups).wait_send()
     for copy in y_send(wx, steps) + y_relay(wx, steps):
         copy.wait_send()
+    for b in range(BATCHES):
+        planes_desc(*z_plane(b)).wait_send()
+        planes_desc(*w_plane(b)).wait_send()
+        for copy in y_send(*z_piece(b)) + y_relay(*z_piece(b)) + w_far(b) + w_near(b):
+            copy.wait_send()
 
 
 def solution(mesh):
@@ -402,12 +559,14 @@
         width = min(CHUNK, depth)
         chunks = depth // width
         slots = groups * CAP
-        steps = BATCHES * chunks
+        steps = BATCHES * (chunks - 1)
         some = groups // BATCHES
         rows = some * CAP
         anywhere = pl.BlockSpec(memory_space=pl.ANY)
         inside = pl.BlockSpec(memory_space=pltpu.VMEM)
         block = pltpu.VMEM((steps, some, CAP, width), BF16)
+        planes = pltpu.VMEM((nodes, groups, CAP, width), BF16)
+        piece = pltpu.VMEM((BATCHES, some, CAP, width), BF16)
         halves = pltpu.VMEM((steps, rows // 2, width), BF16)
         whole = pltpu.VMEM((steps, rows, width), BF16)
         return pl.pallas_call(
@@ -438,10 +597,21 @@
                 whole,
                 block,
                 block,
+                planes,
+                planes,
+                planes,
+                planes,
+                pltpu.VMEM((BATCHES, some // 2, CAP, width), BF16),
+                pltpu.VMEM((BATCHES, some // 2, CAP, width), BF16),
+                piece,
+                piece,
+                piece,
+                piece,
                 pltpu.VMEM((chunks, rows_tok, width), BF16),
                 pltpu.VMEM((slots, rows_tok), BF16),
                 pltpu.VMEM((rows_tok, slots), BF16),
-                pltpu.SemaphoreType.DMA((N_SEMS, steps + 1)),
+                pltpu.SemaphoreType.DMA((N_SEMS, steps + 1 + BATCHES)),
+                pltpu.SemaphoreType.REGULAR((4,)),
             ],
             compiler_params=pltpu.CompilerParams(
                 collective_id=0, has_side_effects=True, vmem_limit_bytes=67043328

time: 148 us -> 143 us (0.966)
  Pallas kernels: 145 us -> 139 us
    pallas_call x1, Pallas kernels: 145 us -> 139 us  [shards(): pl.pallas_call(functools.partial(layer, nodes, groups), out_shape=jax.Sha...]
where the time goes in v2:
time: 143 us; the launch traced here: 142 us
  Pallas kernels  139 us (97%)
  local copies, waits for them, and re-layouts  2.85 us (2%)
    pallas_call x1, Pallas kernels, shards(): pl.pallas_call(functools.partial(layer, nodes, groups), out_shape=jax.Sha...  139 us

profile of v2, /device:TPU:1, one launch (start us, length us, event | category | flops | bytes accessed | tf_op | source)
XLA Modules:
  0.0 142.3 jit_solution(18230202311828775892)
XLA Ops:
  0.0 139.5 %shard_map.64 = bf16[128,7168]{1,0:T(8,128)(2,1)} custom-call(bf16[128,7168]{1,0:T(8,128)(2,1)} %tok_hbm.1, s32[8,128]{1,0:T(8,128)} %bitcast.4, bf16[8,128]{1,0:T(8,128)(2,1)} %bitcast.5, bf16[2,7168,256]{2,1,0:T(8,128)(2,1)} %wg_hbm.1, bf16[2,7168,256]{2,1,0:T(8,128)(2,1)} %wu_hbm.1, bf16[512,7168]{1,0:T(8,128)(2,1)} %bitcast.3), custom_call_target="tpu_custom_call" | custom-call | tf_op jit(solution)/shard_map/pallas_call | solution.py:572
  139.5 2.8 %copy.8 = bf16[128,7168]{1,0:T(8,128)(2,1)} copy(bf16[128,7168]{1,0:T(8,128)(2,1)} %shard_map.64) | data formatting | bytes 3670016

commit v3 on v2

--- a/solution.py
+++ b/solution.py
@@ -13,6 +13,7 @@
 LANES = 128
 CHUNK = 1024
 BATCHES = 2
+EARLY = 4
 MESH = pl.DeviceIdType.MESH
 F32 = jnp.float32
 BF16 = jnp.bfloat16
@@ -35,7 +36,7 @@
     wg_hbm,
     wu_hbm,
     wd_hbm,
-    out_hbm,
+    out_ref,
     tok,
     wg,
     wu,
@@ -68,11 +69,10 @@
     wnl,
     wnr_in,
     wnl_in,
-    outv,
     place_ref,
     place_t_ref,
     sems,
-    round_sems,
+    round_sem,
 ):
     chunks, rows_tok, width = tok.shape
     plain = chunks - 1
@@ -132,21 +132,13 @@
         z, x, core = lax.rem(me_z + dz, deep), lax.rem(me_x + dx, across), lax.rem(me_core + dc, 2)
         return (me_n, (z * across + x) * 2 + core)
 
-    partner = [torus_peer(0, 0, 1)]
-    along_x = [torus_peer(0, 1, 0), torus_peer(0, across - 1, 0)]
-    along_z = [torus_peer(1, 0, 0), torus_peer(deep - 1, 0, 0)] if deep > 1 else []
+    beside = [torus_peer(0, dx, 0) for dx in range(1, across)]
+    greeted = [right, left, torus_peer(0, 0, 1)] + beside
+    greeted += [torus_peer(0, dx, 1) for dx in range(1, across)]
+    greeted += [torus_peer(dz, 0, dc) for dz in range(1, deep) for dc in range(2)]
     barrier = pltpu.get_barrier_semaphore()
-    greeted = [right, left] + partner + along_x + along_z
     for device in greeted:
         pl.semaphore_signal(barrier, inc=1, device_id=device, device_id_type=MESH)
-    rounds = [along_x] + [along_z] * (2 if deep > 1 else 0) + [partner]
-
-    def tell(k):
-        for device in rounds[k]:
-            pl.semaphore_signal(round_sems.at[k], inc=1, device_id=device, device_id_type=MESH)
-
-    def told(k):
-        pl.semaphore_wait(round_sems.at[k], len(rounds[k]))
 
     def tok_copy(c):
         return pltpu.make_async_copy(
@@ -418,13 +410,6 @@
         rsb[u] = part.reshape(some, CAP, width).astype(BF16)
         spread(rsb.at[u], rrb.at[u], sems.at[RS, u], sems.at[RR, u], u // plain)
 
-    def out_copy(c):
-        return pltpu.make_async_copy(
-            outv.at[c],
-            out_hbm.at[:, pl.ds(pl.multiple_of(c * width, width), width)],
-            sems.at[OUT, c],
-        )
-
     def collect(c):
         total = jnp.zeros((rows_tok, width), F32)
         for b in range(BATCHES):
@@ -435,8 +420,7 @@
             if b == 0:
                 rrb[u, 0] = rsb[u, 0]
             total += dot(place_t_ref[:, b * rows : (b + 1) * rows], flat(rrb[u]))
-        outv[c] = total.astype(BF16)
-        out_copy(c).start()
+        out_ref[:, pl.ds(pl.multiple_of(c * width, width), width)] = total.astype(BF16)
 
     prepare(0)
     pl.semaphore_wait(barrier, len(greeted))
@@ -444,19 +428,20 @@
         for copy in y_send(*z_piece(b)):
             copy.start()
     acc[...] = jnp.zeros_like(acc)
-    for c in range(1, chunks):
-        if c <= len(rounds):
-            tell(c - 1)
+    for device in beside:
+        pl.semaphore_signal(round_sem, inc=1, device_id=device, device_id_type=MESH)
+    prepare(1)
+    pl.semaphore_wait(round_sem, len(beside))
+    for c in range(2, chunks):
+        if c - 2 < EARLY:
+            send_plane(c - 2)
         prepare(c)
-        if c <= len(rounds):
-            told(c - 1)
-    for u in range(4):
-        send_plane(u)
+        if c == 4:
+            pass_on(*z_piece(0))
     for b in range(BATCHES):
         at = pl.ds(b * some, some)
         spread(wsb.at[at], wrb.at[at], sems.at[PS, steps], sems.at[PR, steps], b)
-    for b in range(BATCHES):
-        pass_on(*z_piece(b))
+    pass_on(*z_piece(1))
 
     lag_y, lag_x, lag_m = 0, 2, 4
     lag_o = steps + 1
@@ -494,24 +479,23 @@
 
     def w_last():
         total = w_finish(0) + w_finish(1)
-        outv[plain] = total.astype(BF16)
-        out_copy(plain).start()
+        out_ref[:, plain * width :] = total.astype(BF16)
 
     def send_two(k):
-        send_plane(4 + 2 * k)
-        send_plane(5 + 2 * k)
+        send_plane(EARLY + 2 * k)
+        send_plane(EARLY + 1 + 2 * k)
 
     def whole(s, carry):
-        stage(s, 0, 0, (steps - 4) // 2, send_two)
+        stage(s, 0, 0, (steps - EARLY) // 2, send_two)
         stage(s, lag_y, 0, steps, arrive)
-        at_step(s, 1, share_weights)
+        at_step(s, 3, share_weights)
         at_step(s, 3, have_gate_up)
         stage(s, lag_x, 0, steps, lambda u: pass_on(xbuf.at[u], u))
-        at_step(s, 3, pass_on, wx, steps)
+        at_step(s, 5, pass_on, wx, steps)
         at_step(s, 4, z_out, 0)
         at_step(s, 5, z_out, 1)
         stage(s, lag_m, 0, steps, multiply)
-        at_step(s, 6, have_weights)
+        at_step(s, 8, have_weights)
         at_step(s, steps, turn, 0)
         at_step(s, lag_m + steps - 1, turn, 1)
         stage(s, lag_o, 0, steps, start_opposite)
@@ -532,10 +516,6 @@
         spread_wait(rsb.at[u], rrb.at[u], sems.at[RS, u], sems.at[RR, u], u // plain, False)
         for copy in y_send(xbuf.at[u], u) + y_relay(xbuf.at[u], u) + opposite(u) + neighbour(u):
             copy.wait_send()
-
-        @pl.when(u < chunks)
-        def _():
-            out_copy(u).wait()
 
         return carry
 
@@ -571,9 +551,9 @@
         whole = pltpu.VMEM((steps, rows, width), BF16)
         return pl.pallas_call(
             functools.partial(layer, nodes, groups),
-            out_shape=jax.ShapeDtypeStruct((rows_tok, depth), BF16),
+            out_shape=pltpu.VMEM((rows_tok, depth), BF16),
             in_specs=[anywhere, inside, inside, anywhere, anywhere, anywhere],
-            out_specs=anywhere,
+            out_specs=inside,
             scratch_shapes=[
                 pltpu.VMEM((chunks, rows_tok, width), BF16),
                 pltpu.VMEM(w_gate.shape, BF16),
@@ -607,14 +587,13 @@
                 piece,
                 piece,
                 piece,
-                pltpu.VMEM((chunks, rows_tok, width), BF16),
                 pltpu.VMEM((slots, rows_tok), BF16),
                 pltpu.VMEM((rows_tok, slots), BF16),
                 pltpu.SemaphoreType.DMA((N_SEMS, steps + 1 + BATCHES)),
-                pltpu.SemaphoreType.REGULAR((4,)),
+                pltpu.SemaphoreType.REGULAR,
             ],
             compiler_params=pltpu.CompilerParams(
-                collective_id=0, has_side_effects=True, vmem_limit_bytes=67043328
+                collective_id=0, has_side_effects=True, vmem_limit_bytes=58500000
             ),
         )(
             tokens,

time: 143 us -> 139 us (0.972)
  local copies, waits for them, and re-layouts: 2.85 us -> 1.23 us
    pallas_call x1, Pallas kernels: 139 us -> 138 us  [shards(): pl.pallas_call(functools.partial(layer, nodes, groups), out_shape=pltpu.V...]
    unnamed x1, local copies, waits for them, and re-layouts: 2.85 us -> 1.23 us
where the time goes in v3:
time: 139 us
  Pallas kernels  138 us (99%)
    pallas_call x1, Pallas kernels, shards(): pl.pallas_call(functools.partial(layer, nodes, groups), out_shape=pltpu.V...  138 us

profile of v3, /device:TPU:1, one launch (start us, length us, event | category | flops | bytes accessed | tf_op | source)
XLA Modules:
  0.0 138.8 jit_solution(6712115328324615024)
XLA Ops:
  0.0 137.6 %shard_map.64 = bf16[128,7168]{1,0:T(8,128)(2,1)S(1)} custom-call(bf16[128,7168]{1,0:T(8,128)(2,1)} %tok_hbm.1, s32[8,128]{1,0:T(8,128)} %bitcast.4, bf16[8,128]{1,0:T(8,128)(2,1)} %bitcast.5, bf16[2,7168,256]{2,1,0:T(8,128)(2,1)} %wg_hbm.1, bf16[2,7168,256]{2,1,0:T(8,128)(2,1)} %wu_hbm.1, bf16[512,7168]{1,0:T(8,128)(2,1)} %bitcast.3), custom_call_target="tpu_custom_call" | custom-call | tf_op jit(solution)/shard_map/pallas_call | solution.py:552
  137.6 1.2 copy.8

commit v4 on v3

--- a/solution.py
+++ b/solution.py
@@ -14,6 +14,7 @@
 CHUNK = 1024
 BATCHES = 2
 EARLY = 4
+PACK = 16
 MESH = pl.DeviceIdType.MESH
 F32 = jnp.float32
 BF16 = jnp.bfloat16
@@ -31,12 +32,14 @@
     nodes,
     groups,
     tok_hbm,
-    ids_ref,
-    rw_ref,
+    ids_hbm,
+    rw_hbm,
     wg_hbm,
     wu_hbm,
     wd_hbm,
     out_ref,
+    ids_ref,
+    rw_ref,
     tok,
     wg,
     wu,
@@ -47,6 +50,7 @@
     wsb,
     wrb,
     wx,
+    wcol,
     acc,
     hid,
     opr,
@@ -156,6 +160,10 @@
 
     wg_copy = pltpu.make_async_copy(wg_hbm, wg, sems.at[TOK, chunks])
     wu_copy = pltpu.make_async_copy(wu_hbm, wu, sems.at[WT, chunks])
+    ids_copy = pltpu.make_async_copy(ids_hbm, ids_ref, sems.at[OUT, 0])
+    rw_copy = pltpu.make_async_copy(rw_hbm, rw_ref, sems.at[OUT, 1])
+    ids_copy.start()
+    rw_copy.start()
     for c in range(chunks):
         tok_copy(c).start()
     wg_copy.start()
@@ -167,6 +175,8 @@
     spot = slot // CAP
     offset = BATCHES * lax.rem(spot, some) + spot // some
     group = lax.rem(me_t + offset, groups)
+    ids_copy.wait()
+    rw_copy.wait()
     ids = ids_ref[...]
     weights = rw_ref[...].astype(F32)
     member = jnp.zeros((slots, rows_tok), F32)
@@ -356,11 +366,10 @@
         )
 
     def activate(batch):
-        w_all = wx[:, pl.ds(pl.multiple_of(batch * rows, rows), rows), :]
-        w_all = w_all.astype(F32).reshape(nodes * rows, LANES)
         for e in range(EXP_DEV):
             gate = acc[batch, 2 * e]
-            gain = jnp.broadcast_to(w_all[:, e * (LANES // 2) : e * (LANES // 2) + 1], gate.shape)
+            gain = wcol[e, :, batch * rows : (batch + 1) * rows, :].reshape(nodes * rows, LANES)
+            gain = jnp.broadcast_to(gain[:, :1], gate.shape)
             value = gate / (1.0 + jnp.exp(-gate)) * acc[batch, 2 * e + 1] * gain
             hid[batch, :, e * ff : (e + 1) * ff] = value.astype(BF16)
 
@@ -441,6 +450,7 @@
     for b in range(BATCHES):
         at = pl.ds(b * some, some)
         spread(wsb.at[at], wrb.at[at], sems.at[PS, steps], sems.at[PR, steps], b)
+    arrive(0)
     pass_on(*z_piece(1))
 
     lag_y, lag_x, lag_m = 0, 2, 4
@@ -460,7 +470,10 @@
     def share_weights():
         spread_desc(wsb, wrb, sems.at[PS, steps], sems.at[PR, steps], 1, groups).wait_recv()
         wrb[0] = wsb[0]
-        wx[OWN] = flat(wrb[...])
+        turned = jnp.transpose(wrb[...].astype(F32).reshape(slots, LANES)).astype(BF16)
+        for e in range(EXP_DEV):
+            first = e * (LANES // EXP_DEV)
+            wx[OWN, e * PACK : (e + 1) * PACK] = turned[first : first + PACK]
         for copy in y_send(wx, steps):
             copy.start()
 
@@ -471,6 +484,10 @@
     def have_weights():
         for copy in y_relay(wx, steps):
             copy.wait_recv()
+        for e in range(EXP_DEV):
+            for plane in range(nodes):
+                line = wx[plane, e * PACK : e * PACK + 1, :].astype(F32)
+                wcol[e, plane] = jnp.transpose(jnp.broadcast_to(line, (LANES, slots)))
 
     def turn(batch):
         z_multiply(batch)
@@ -487,7 +504,7 @@
 
     def whole(s, carry):
         stage(s, 0, 0, (steps - EARLY) // 2, send_two)
-        stage(s, lag_y, 0, steps, arrive)
+        stage(s, lag_y, 1, steps, arrive)
         at_step(s, 3, share_weights)
         at_step(s, 3, have_gate_up)
         stage(s, lag_x, 0, steps, lambda u: pass_on(xbuf.at[u], u))
@@ -552,9 +569,11 @@
         return pl.pallas_call(
             functools.partial(layer, nodes, groups),
             out_shape=pltpu.VMEM((rows_tok, depth), BF16),
-            in_specs=[anywhere, inside, inside, anywhere, anywhere, anywhere],
+            in_specs=[anywhere] * 6,
             out_specs=inside,
             scratch_shapes=[
+                pltpu.VMEM(expert_ids.shape[::-1], jnp.int32),
+                pltpu.VMEM(route_weight.shape[::-1], BF16),
                 pltpu.VMEM((chunks, rows_tok, width), BF16),
                 pltpu.VMEM(w_gate.shape, BF16),
                 pltpu.VMEM(w_up.shape, BF16),
@@ -564,7 +583,8 @@
                 pltpu.VMEM((steps, nodes, rows, width), BF16),
                 pltpu.VMEM((groups, CAP, LANES), BF16),
                 pltpu.VMEM((groups, CAP, LANES), BF16),
-                pltpu.VMEM((nodes, slots, LANES), BF16),
+                pltpu.VMEM((nodes, EXP_DEV * PACK, slots), BF16),
+                pltpu.VMEM((EXP_DEV, nodes, slots, LANES), F32),
                 pltpu.VMEM((BATCHES, 2 * EXP_DEV, nodes * rows, ff), F32),
                 pltpu.VMEM((BATCHES, nodes * rows, EXP_DEV * ff), BF16),
                 halves,
@@ -593,7 +613,7 @@
                 pltpu.SemaphoreType.REGULAR,
             ],
             compiler_params=pltpu.CompilerParams(
-                collective_id=0, has_side_effects=True, vmem_limit_bytes=58500000
+                collective_id=0, has_side_effects=True, vmem_limit_bytes=59000000
             ),
         )(
             tokens,

time: 139 us -> 137 us (0.986)
  Pallas kernels: 138 us -> 136 us
    pallas_call x1, Pallas kernels: 138 us -> 136 us  [shards(): pl.pallas_call(functools.partial(layer, nodes, groups), out_shape=pltpu.V...]
where the time goes in v4:
time: 137 us
  Pallas kernels  136 us (99%)
    pallas_call x1, Pallas kernels, shards(): pl.pallas_call(functools.partial(layer, nodes, groups), out_shape=pltpu.V...  136 us

profile of v4, /device:TPU:1, one launch (start us, length us, event | category | flops | bytes accessed | tf_op | source)
XLA Modules:
  0.0 137.0 jit_solution(15388311632353053373)
XLA Ops:
  0.0 135.8 %shard_map.64 = bf16[128,7168]{1,0:T(8,128)(2,1)S(1)} custom-call(bf16[128,7168]{1,0:T(8,128)(2,1)} %tok_hbm.1, s32[8,128]{1,0:T(8,128)} %bitcast.4, bf16[8,128]{1,0:T(8,128)(2,1)} %bitcast.5, bf16[2,7168,256]{2,1,0:T(8,128)(2,1)} %wg_hbm.1, bf16[2,7168,256]{2,1,0:T(8,128)(2,1)} %wu_hbm.1, bf16[512,7168]{1,0:T(8,128)(2,1)} %bitcast.3), custom_call_target="tpu_custom_call" | custom-call | tf_op jit(solution)/shard_map/pallas_call | solution.py:569
  135.8 1.2 copy.8

commit v5 on v4

v5 whole, which is shorter than its diff:
```python
import functools

import jax
import jax.numpy as jnp
from jax import lax
from jax.experimental import pallas as pl
from jax.experimental.pallas import tpu as pltpu
from jax.sharding import PartitionSpec as P

EXP_DEV = 2
CAP = 4
QBLOCK = 128
LANES = 128
CHUNK = 1024
BATCHES = 2
EARLY = 4
PACK = 16
MESH = pl.DeviceIdType.MESH
F32 = jnp.float32
BF16 = jnp.bfloat16

(
    TOK_FIRST,
    TOK_REST,
    W_GATE,
    W_UP,
    W_DOWN,
    IDS,
    GAINS,
    PLANE_SENT,
    GAIN_PLANE_SENT,
    Z_PLANE_SENT,
    Y_SENT,
    RELAY_SENT,
    GAIN_Y_SENT,
    GAIN_RELAY_SENT,
    Z_Y_SENT,
    Z_RELAY_SENT,
    OPP_SENT,
    NEAR_SENT,
    BACK_SENT,
    W_FAR_SENT,
    W_NEAR_SENT,
    W_PLANE_SENT,
    PLANE_SENT_ODD,
    SINGLES,
) = range(24)


def dot(a, b):
    return jnp.dot(a, b, preferred_element_type=F32)


def layer(
    nodes,
    groups,
    tok_hbm,
    ids_hbm,
    rw_hbm,
    wg_hbm,
    wu_hbm,
    wd_hbm,
    out_ref,
    ids_ref,
    rw_ref,
    tok,
    wg,
    wu,
    wd,
    sbuf,
    rbuf,
    xbuf,
    wsb,
    wrb,
    wx,
    wcol,
    acc,
    hid,
    opp,
    opp_in,
    near,
    near_in,
    rsb,
    rrb,
    zbuf,
    zin,
    wbuf,
    win,
    w_opp_in,
    w_near,
    w_near_in,
    place_ref,
    place_t_ref,
    sems,
    round_sem,
):
    chunks, rows_tok, width = tok.shape
    plain = chunks - 1
    steps = BATCHES * plain
    some = groups // BATCHES
    slots = groups * CAP
    rows = some * CAP
    half = rows // 2
    ff = wg.shape[2]
    me_n = lax.axis_index("node")
    me_t = lax.axis_index("torus")
    right = (lax.rem(me_n + 1, nodes), me_t)
    left = (lax.rem(me_n + nodes - 1, nodes), me_t)
    OWN, RIGHT, LEFT, FAR = range(4)

    table = steps + 1 + BATCHES

    def plane_in(u):
        return sems.at[u]

    def near_sem(u):
        return sems.at[table + u]

    def far_sem(u):
        return sems.at[2 * table + u]

    def back_sem(c):
        return sems.at[3 * table + c]

    def single(k):
        return sems.at[3 * table + plain + BATCHES + k]

    def plane_peer(r):
        return (me_n, lax.rem(me_t + r, groups))

    def remote(src, dst, send, recv, device):
        return pltpu.make_async_remote_copy(
            src_ref=src,
            dst_ref=dst,
            send_sem=send,
            recv_sem=recv,
            device_id=device,
            device_id_type=MESH,
        )

    def spread(src, dst, send, recv, batch, base=0):
        def one(j, carry):
            peer = plane_peer(BATCHES * j + batch)
            remote(src.at[base + j], dst.at[base + some - batch - j], send, recv, peer).start()
            return carry

        lax.fori_loop(1 - batch, some, one, 0)

    def spread_desc(src, dst, send, recv, low, high):
        at = pl.ds(low, high - low)
        return remote(src.at[at], dst.at[at], send, recv, plane_peer(1))

    def plane_sent(batch):
        return single(PLANE_SENT) if batch == 0 else single(PLANE_SENT_ODD)

    across = min(4, groups // 2)
    deep = groups // (2 * across)
    me_core, me_x, me_z = lax.rem(me_t, 2), lax.rem(me_t // 2, across), me_t // (2 * across)

    def torus_peer(dz, dx, dc):
        z, x, core = lax.rem(me_z + dz, deep), lax.rem(me_x + dx, across), lax.rem(me_core + dc, 2)
        return (me_n, (z * across + x) * 2 + core)

    beside = [torus_peer(0, dx, 0) for dx in range(1, across)]
    greeted = [right, left, torus_peer(0, 0, 1)] + beside
    greeted += [torus_peer(0, dx, 1) for dx in range(1, across)]
    greeted += [torus_peer(dz, 0, dc) for dz in range(1, deep) for dc in range(2)]
    barrier = pltpu.get_barrier_semaphore()
    for device in greeted:
        pl.semaphore_signal(barrier, inc=1, device_id=device, device_id_type=MESH)

    def tok_copy(c):
        return pltpu.make_async_copy(
            tok_hbm.at[:, pl.ds(pl.multiple_of(c * width, width), width)],
            tok.at[c],
            single(TOK_FIRST if c == 0 else TOK_REST),
        )

    def wd_copy(c):
        return pltpu.make_async_copy(
            wd_hbm.at[:, pl.ds(pl.multiple_of(c * width, width), width)], wd.at[c], single(W_DOWN)
        )

    wg_copy = pltpu.make_async_copy(wg_hbm, wg, single(W_GATE))
    wu_copy = pltpu.make_async_copy(wu_hbm, wu, single(W_UP))
    ids_copy = pltpu.make_async_copy(ids_hbm, ids_ref, single(IDS))
    rw_copy = pltpu.make_async_copy(rw_hbm, rw_ref, single(GAINS))
    ids_copy.start()
    rw_copy.start()
    for c in range(chunks):
        tok_copy(c).start()
    wg_copy.start()
    wu_copy.start()
    for c in range(chunks):
        wd_copy(c).start()

    slot = lax.broadcasted_iota(jnp.int32, (slots, rows_tok), 0)
    spot = slot // CAP
    offset = BATCHES * lax.rem(spot, some) + spot // some
    group = lax.rem(me_t + offset, groups)
    ids_copy.wait()
    rw_copy.wait()
    ids = ids_ref[...]
    weights = rw_ref[...].astype(F32)
    member = jnp.zeros((slots, rows_tok), F32)
    weight_a = jnp.zeros((slots, rows_tok), F32)
    weight_b = jnp.zeros((slots, rows_tok), F32)
    for k in range(ids.shape[0]):
        one = jnp.broadcast_to(ids[k : k + 1, :], (slots, rows_tok))
        gain = jnp.broadcast_to(weights[k : k + 1, :], (slots, rows_tok))
        is_a = one == 2 * group
        is_b = one == 2 * group + 1
        weight_a = jnp.where(is_a, gain, weight_a)
        weight_b = jnp.where(is_b, gain, weight_b)
        member = jnp.where(is_a | is_b, jnp.float32(1.0), member)
    before = (
        lax.broadcasted_iota(jnp.int32, (rows_tok, rows_tok), 0)
        < lax.broadcasted_iota(jnp.int32, (rows_tok, rows_tok), 1)
    )
    before = jnp.where(before, jnp.float32(1.0), jnp.float32(0.0)).astype(BF16)
    index = dot(member.astype(BF16), before)
    here = index == lax.rem(slot, CAP).astype(F32)
    place = jnp.where(here, member, jnp.float32(0.0))
    place_ref[...] = place.astype(BF16)
    place_t_ref[...] = jnp.transpose(place).astype(BF16)
    lane = lax.broadcasted_iota(jnp.int32, (rows_tok, LANES), 1)
    low = jnp.where(lane < LANES // 2, jnp.float32(1.0), jnp.float32(0.0))
    spread_w = dot((place * weight_a).astype(BF16), low.astype(BF16)) + dot(
        (place * weight_b).astype(BF16), (1.0 - low).astype(BF16)
    )
    wsb[...] = spread_w.reshape(groups, CAP, LANES).astype(BF16)

    def prepare(c):
        if c == 0:
            tok_copy(0).wait()
        elif c == 1:
            rest = tok.at[pl.ds(1, chunks - 1)]
            pltpu.make_async_copy(rest, rest, single(TOK_REST)).wait()
        parts = []
        for b in range(width // QBLOCK):
            x = tok[c, :, b * QBLOCK : (b + 1) * QBLOCK].astype(F32)
            top = jnp.max(jnp.abs(x), axis=1, keepdims=True)
            scale = ((top + 1e-06) * (1.0 / 448.0)).astype(BF16).astype(F32)
            scale = jnp.broadcast_to(scale, x.shape)
            quantized = (x / scale).astype(BF16)
            parts.append((quantized.astype(F32) * scale).astype(BF16))
        restored = jnp.concatenate(parts, axis=1)
        picked = dot(place_ref[...], restored).reshape(groups, CAP, width).astype(BF16)
        if c == 0:
            zbuf[OWN] = picked
        else:
            for b in range(BATCHES):
                sbuf[b * plain + c - 1] = picked[b * some : (b + 1) * some]

    def send_plane(u):
        if isinstance(u, int):
            spread(sbuf.at[u], rbuf.at[u], plane_sent(u // plain), plane_in(u), u // plain)
            return
        for b in range(BATCHES):

            @pl.when(u // plain == b)
            def _(b=b):
                spread(sbuf.at[u], rbuf.at[u], plane_sent(b), plane_in(u), b)

    def y_send(block, u, sent):
        return (
            remote(block.at[OWN], block.at[LEFT], single(sent), near_sem(u), right),
            remote(block.at[OWN], block.at[RIGHT], single(sent), near_sem(u), left),
        )

    def y_relay(block, u, sent):
        middle = block.shape[1] // 2
        low, high = pl.ds(0, middle), pl.ds(middle, middle)
        return (
            remote(block.at[LEFT, low], block.at[FAR, low], single(sent), far_sem(u), right),
            remote(block.at[RIGHT, high], block.at[FAR, high], single(sent), far_sem(u), left),
        )

    def wait_in(ref, sem):
        remote(ref, ref, single(Y_SENT), sem, right).wait_recv()

    def wait_out(ref, k):
        remote(ref, ref, single(k), near_sem(0), right).wait_send()

    def wait_far(block, u):
        wait_in(block.at[FAR], far_sem(u))

    def flat(ref_value):
        count, cap, lanes = ref_value.shape
        return ref_value.astype(F32).reshape(count * cap, lanes).astype(BF16)

    def arrive(u):
        def gather(low, high):
            wait_in(rbuf.at[u, pl.ds(low, high - low)], plane_in(u))

        def own_too():
            gather(1, some)
            rbuf[u, 0] = sbuf[u, 0]

        if isinstance(u, int):
            own_too()
        else:
            pl.when(u // plain == 0)(own_too)
            pl.when(u // plain == 1)(lambda: gather(0, some))
        xbuf[u, OWN] = flat(rbuf[u])
        for copy in y_send(xbuf.at[u], u, Y_SENT):
            copy.start()

    def pass_on(block, u, sent):
        wait_in(block.at[pl.ds(RIGHT, 2)], near_sem(u))
        for copy in y_relay(block, u, sent):
            copy.start()

    def multiply(u):
        wait_far(xbuf.at[u], u)
        batch = u // plain
        add_chunk(xbuf[u].reshape(nodes * rows, width), batch, u - batch * plain + 1)

    def add_chunk(x, batch, c):
        at = pl.ds(pl.multiple_of(c * width, width), width)
        for e in range(EXP_DEV):
            acc[batch, 2 * e] += dot(x, wg[e, at, :])
            acc[batch, 2 * e + 1] += dot(x, wu[e, at, :])

    def z_piece(batch):
        return zbuf.at[:, pl.ds(batch * some, some)], steps + 1 + batch

    def spread_planes(src, dst, send, recv, batch):
        def one(j, carry):
            peer = plane_peer(BATCHES * j + batch)
            here, there = batch * some + j, batch * some + some - batch - j
            remote(src.at[:, here], dst.at[:, there], send, recv, peer).start()
            return carry

        lax.fori_loop(1 - batch, some, one, 0)

    def wait_planes(ref, sem, batch):
        wait_in(ref.at[:, pl.ds(batch * some + 1 - batch, some - 1 + batch)], sem)

    def z_out(batch):
        wait_far(*z_piece(batch))
        spread_planes(zbuf, zin, single(Z_PLANE_SENT), plane_in(steps + 1 + batch), batch)

    def z_multiply(batch):
        wait_planes(zin, plane_in(steps + 1 + batch), batch)
        if batch == 0:
            zin[:, 0] = zbuf[:, 0]
        x = zin[:, batch * some : (batch + 1) * some].astype(F32)
        add_chunk(x.reshape(nodes * rows, width).astype(BF16), batch, 0)

    def w_project(batch):
        part = dot(hid[batch], wd[plain])
        wbuf[:, batch * some : (batch + 1) * some] = part.reshape(nodes, some, CAP, width).astype(BF16)
        spread_planes(wbuf, win, single(W_PLANE_SENT), back_sem(plain + batch), batch)

    def w_opposite(batch):
        wait_planes(win, back_sem(plain + batch), batch)
        if batch == 0:
            win[:, 0] = wbuf[:, 0]
        mid = some // 2
        for k, device in enumerate((right, left)):
            part = win.at[FAR, pl.ds(batch * some + k * mid, mid)]
            sem = near_sem(steps + 1 + batch)
            remote(part, w_opp_in.at[batch, k], single(W_FAR_SENT), sem, device).start()

    def w_neighbour(batch):
        low, mid, high = batch * some, batch * some + some // 2, (batch + 1) * some
        wait_in(w_opp_in.at[batch], near_sem(steps + 1 + batch))
        w_near[batch, 0, : some // 2] = (
            win[RIGHT, low:mid].astype(F32) + w_opp_in[batch, 0].astype(F32)
        ).astype(BF16)
        w_near[batch, 0, some // 2 :] = win[RIGHT, mid:high]
        w_near[batch, 1, : some // 2] = win[LEFT, low:mid]
        w_near[batch, 1, some // 2 :] = (
            win[LEFT, mid:high].astype(F32) + w_opp_in[batch, 1].astype(F32)
        ).astype(BF16)
        for k, device in enumerate((right, left)):
            sem = far_sem(steps + 1 + batch)
            remote(w_near.at[batch, k], w_near_in.at[batch, k], single(W_NEAR_SENT), sem, device).start()

    def w_finish(batch):
        wait_in(w_near_in.at[batch], far_sem(steps + 1 + batch))
        part = win[OWN, batch * some : (batch + 1) * some].astype(F32)
        part = part + w_near_in[batch, 0].astype(F32) + w_near_in[batch, 1].astype(F32)
        return dot(
            place_t_ref[:, batch * rows : (batch + 1) * rows], part.reshape(rows, width).astype(BF16)
        )

    def activate(batch):
        for e in range(EXP_DEV):
            gate = acc[batch, 2 * e]
            gain = wcol[e, :, batch * rows : (batch + 1) * rows, :].reshape(nodes * rows, LANES)
            gain = jnp.broadcast_to(gain[:, :1], gate.shape)
            value = gate / (1.0 + jnp.exp(-gate)) * acc[batch, 2 * e + 1] * gain
            hid[batch, :, e * ff : (e + 1) * ff] = value.astype(BF16)

    def project(u, first, count):
        batch = u // plain
        return dot(hid[batch, first * rows : (first + count) * rows, :], wd[u - batch * plain])

    def start_opposite(u):
        part = project(u, FAR, 1)
        for k, device in enumerate((right, left)):
            opp[u, k] = part[k * half : (k + 1) * half].astype(BF16)
            remote(opp.at[u, k], opp_in.at[u, k], single(OPP_SENT), near_sem(u), device).start()

    def start_neighbour(u):
        part = project(u, RIGHT, 2)
        wait_in(opp_in.at[u], near_sem(u))
        near[u, 0, :half] = (part[:half] + opp_in[u, 0].astype(F32)).astype(BF16)
        near[u, 0, half:] = part[half:rows].astype(BF16)
        near[u, 1, :half] = part[rows : rows + half].astype(BF16)
        near[u, 1, half:] = (part[rows + half :] + opp_in[u, 1].astype(F32)).astype(BF16)
        for k, device in enumerate((right, left)):
            remote(near.at[u, k], near_in.at[u, k], single(NEAR_SENT), far_sem(u), device).start()

    def finish(u):
        part = project(u, OWN, 1)
        wait_in(near_in.at[u], far_sem(u))
        part = part + near_in[u, 0].astype(F32) + near_in[u, 1].astype(F32)
        batch = u // plain
        c, base = u - batch * plain, batch * some
        rsb[c, pl.ds(base, some)] = part.reshape(some, CAP, width).astype(BF16)
        spread(rsb.at[c], rrb.at[c], single(BACK_SENT), back_sem(c), batch, base)

    def collect(c):
        wait_in(rrb.at[c, pl.ds(1, groups - 1)], back_sem(c))
        rrb[c, 0] = rsb[c, 0]
        total = jnp.zeros((rows_tok, width), F32)
        for b in range(BATCHES):
            back = flat(rrb[c, b * some : (b + 1) * some])
            total += dot(place_t_ref[:, b * rows : (b + 1) * rows], back)
        out_ref[:, pl.ds(pl.multiple_of(c * width, width), width)] = total.astype(BF16)

    prepare(0)
    pl.semaphore_wait(barrier, len(greeted))
    for b in range(BATCHES):
        for copy in y_send(*z_piece(b), Z_Y_SENT):
            copy.start()
    acc[...] = jnp.zeros_like(acc)
    for device in beside:
        pl.semaphore_signal(round_sem, inc=1, device_id=device, device_id_type=MESH)
    prepare(1)
    pl.semaphore_wait(round_sem, len(beside))
    for c in range(2, chunks):
        if c - 2 < EARLY:
            send_plane(c - 2)
        prepare(c)
        if c == 4:
            pass_on(*z_piece(0), Z_RELAY_SENT)
    for b in range(BATCHES):
        at = pl.ds(b * some, some)
        spread(wsb.at[at], wrb.at[at], single(GAIN_PLANE_SENT), plane_in(steps), b)
    arrive(0)
    pass_on(*z_piece(1), Z_RELAY_SENT)

    lag_y, lag_x, lag_m = 0, 2, 4
    lag_o = steps + 1
    lag_n, lag_f, lag_c = lag_o + 2, lag_o + 4, lag_o + 6

    def stage(s, lag, first, last, work):
        @pl.when((s >= lag + first) & (s < lag + last))
        def _():
            work(s - lag)

    def at_step(s, step, work, *args):
        @pl.when(s == step)
        def _():
            work(*args)

    def share_weights():
        wait_in(wrb.at[pl.ds(1, groups - 1)], plane_in(steps))
        wrb[0] = wsb[0]
        turned = jnp.transpose(wrb[...].astype(F32).reshape(slots, LANES)).astype(BF16)
        for e in range(EXP_DEV):
            first = e * (LANES // EXP_DEV)
            wx[OWN, e * PACK : (e + 1) * PACK] = turned[first : first + PACK]
        for copy in y_send(wx, steps, GAIN_Y_SENT):
            copy.start()

    def have_gate_up():
        wg_copy.wait()
        wu_copy.wait()
        pltpu.make_async_copy(wd, wd, single(W_DOWN)).wait()

    def have_weights():
        wait_far(wx, steps)
        for e in range(EXP_DEV):
            for plane in range(nodes):
                line = wx[plane, e * PACK : e * PACK + 1, :].astype(F32)
                wcol[e, plane] = jnp.transpose(jnp.broadcast_to(line, (LANES, slots)))

    def turn(batch):
        z_multiply(batch)
        activate(batch)
        w_project(batch)

    def w_last():
        total = w_finish(0) + w_finish(1)
        out_ref[:, plain * width :] = total.astype(BF16)

    def send_two(k):
        send_plane(EARLY + 2 * k)
        send_plane(EARLY + 1 + 2 * k)

    def whole(s, carry):
        stage(s, 0, 0, (steps - EARLY) // 2, send_two)
        stage(s, lag_y, 1, steps, arrive)
        at_step(s, 3, share_weights)
        at_step(s, 3, have_gate_up)
        stage(s, lag_x, 0, steps, lambda u: pass_on(xbuf.at[u], u, RELAY_SENT))
        at_step(s, 5, pass_on, wx, steps, GAIN_RELAY_SENT)
        at_step(s, 4, z_out, 0)
        at_step(s, 5, z_out, 1)
        stage(s, lag_m, 0, steps, multiply)
        at_step(s, 8, have_weights)
        at_step(s, steps, turn, 0)
        at_step(s, lag_m + steps - 1, turn, 1)
        stage(s, lag_o, 0, steps, start_opposite)
        at_step(s, lag_o + steps, w_opposite, 0)
        at_step(s, lag_o + steps + 1, w_opposite, 1)
        stage(s, lag_n, 0, steps, start_neighbour)
        at_step(s, lag_n + steps, w_neighbour, 0)
        at_step(s, lag_n + steps + 1, w_neighbour, 1)
        stage(s, lag_f, 0, steps, finish)
        stage(s, lag_c + steps - plain, 0, plain, collect)
        at_step(s, lag_f + steps + 1, w_last)
        return carry

    lax.fori_loop(0, lag_f + steps + 2, whole, 0)

    first, second = pl.ds(0, plain), pl.ds(plain, plain)
    wait_out(sbuf.at[first, pl.ds(1, some - 1)], PLANE_SENT)
    wait_out(sbuf.at[second], PLANE_SENT_ODD)
    wait_out(wsb.at[pl.ds(1, groups - 1)], GAIN_PLANE_SENT)
    wait_out(zbuf.at[:, pl.ds(1, groups - 1)], Z_PLANE_SENT)
    wait_out(wbuf.at[:, pl.ds(1, groups - 1)], W_PLANE_SENT)
    wait_out(rsb.at[:, pl.ds(1, groups - 1)], BACK_SENT)
    wait_out(xbuf.at[:, pl.ds(RIGHT, 2)], Y_SENT)
    wait_out(xbuf.at[:, FAR], RELAY_SENT)
    wait_out(wx.at[pl.ds(RIGHT, 2)], GAIN_Y_SENT)
    wait_out(wx.at[FAR], GAIN_RELAY_SENT)
    wait_out(zbuf.at[pl.ds(RIGHT, 2)], Z_Y_SENT)
    wait_out(zbuf.at[FAR], Z_RELAY_SENT)
    wait_out(opp, OPP_SENT)
    wait_out(near, NEAR_SENT)
    wait_out(w_opp_in, W_FAR_SENT)
    wait_out(w_near, W_NEAR_SENT)


def solution(mesh):
    nodes, groups = mesh.shape["node"], mesh.shape["torus"]

    def shards(tokens, expert_ids, route_weight, w_gate, w_up, w_down):
        rows_tok, depth = tokens.shape
        ff = w_gate.shape[2]
        width = min(CHUNK, depth)
        chunks = depth // width
        slots = groups * CAP
        steps = BATCHES * (chunks - 1)
        some = groups // BATCHES
        rows = some * CAP
        anywhere = pl.BlockSpec(memory_space=pl.ANY)
        inside = pl.BlockSpec(memory_space=pltpu.VMEM)
        block = pltpu.VMEM((steps, some, CAP, width), BF16)
        planes = pltpu.VMEM((nodes, groups, CAP, width), BF16)
        piece = pltpu.VMEM((BATCHES, 2, some, CAP, width), BF16)
        returned = pltpu.VMEM((chunks - 1, groups, CAP, width), BF16)
        arrivals = 3 * (steps + 1 + BATCHES) + chunks - 1 + BATCHES
        return pl.pallas_call(
            functools.partial(layer, nodes, groups),
            out_shape=pltpu.VMEM((rows_tok, depth), BF16),
            in_specs=[anywhere] * 6,
            out_specs=inside,
            scratch_shapes=[
                pltpu.VMEM(expert_ids.shape[::-1], jnp.int32),
                pltpu.VMEM(route_weight.shape[::-1], BF16),
                pltpu.VMEM((chunks, rows_tok, width), BF16),
                pltpu.VMEM(w_gate.shape, BF16),
                pltpu.VMEM(w_up.shape, BF16),
                pltpu.VMEM((chunks, EXP_DEV * ff, width), BF16),
                block,
                block,
                pltpu.VMEM((steps, nodes, rows, width), BF16),
                pltpu.VMEM((groups, CAP, LANES), BF16),
                pltpu.VMEM((groups, CAP, LANES), BF16),
                pltpu.VMEM((nodes, EXP_DEV * PACK, slots), BF16),
                pltpu.VMEM((EXP_DEV, nodes, slots, LANES), F32),
                pltpu.VMEM((BATCHES, 2 * EXP_DEV, nodes * rows, ff), F32),
                pltpu.VMEM((BATCHES, nodes * rows, EXP_DEV * ff), BF16),
                pltpu.VMEM((steps, 2, rows // 2, width), BF16),
                pltpu.VMEM((steps, 2, rows // 2, width), BF16),
                pltpu.VMEM((steps, 2, rows, width), BF16),
                pltpu.VMEM((steps, 2, rows, width), BF16),
                returned,
                returned,
                planes,
                planes,
                planes,
                planes,
                pltpu.VMEM((BATCHES, 2, some // 2, CAP, width), BF16),
                piece,
                piece,
                pltpu.VMEM((slots, rows_tok), BF16),
                pltpu.VMEM((rows_tok, slots), BF16),
                pltpu.SemaphoreType.DMA((arrivals + SINGLES,)),
                pltpu.SemaphoreType.REGULAR,
            ],
            compiler_params=pltpu.CompilerParams(
                collective_id=0, has_side_effects=True, vmem_limit_bytes=59000000
            ),
        )(
            tokens,
            expert_ids.T,
            route_weight.T,
            w_gate,
            w_up,
            w_down.reshape(EXP_DEV * ff, depth),
        )

    placed = (
        P(("node", "torus"), None),
        P(("node", "torus"), None),
        P(("node", "torus"), None),
        P("torus", None, "node"),
        P("torus", None, "node"),
        P("torus", "node", None),
    )
    return jax.shard_map(
        shards, mesh=mesh, in_specs=placed, out_specs=P(("node", "torus"), None), check_vma=False
    )
```

time: 137 us -> 134 us (0.978)
  Pallas kernels: 136 us -> 133 us
    pallas_call x1, Pallas kernels: 136 us -> 133 us  [shards(): pl.pallas_call(functools.partial(layer, nodes, groups), out_shape=pltpu.V...]
where the time goes in v5:
time: 134 us
  Pallas kernels  133 us (99%)
    pallas_call x1, Pallas kernels, shards(): pl.pallas_call(functools.partial(layer, nodes, groups), out_shape=pltpu.V...  133 us

profile of v5, /device:TPU:1, one launch (start us, length us, event | category | flops | bytes accessed | tf_op | source)
XLA Modules:
  0.0 134.3 jit_solution(4658930800655908563)
XLA Ops:
  0.0 133.0 %shard_map.64 = bf16[128,7168]{1,0:T(8,128)(2,1)S(1)} custom-call(bf16[128,7168]{1,0:T(8,128)(2,1)} %tok_hbm.1, s32[8,128]{1,0:T(8,128)} %bitcast.4, bf16[8,128]{1,0:T(8,128)(2,1)} %bitcast.5, bf16[2,7168,256]{2,1,0:T(8,128)(2,1)} %wg_hbm.1, bf16[2,7168,256]{2,1,0:T(8,128)(2,1)} %wu_hbm.1, bf16[512,7168]{1,0:T(8,128)(2,1)} %bitcast.3), custom_call_target="tpu_custom_call" | custom-call | tf_op jit(solution)/shard_map/pallas_call | solution.py:570
  133.0 1.2 copy.8

commit v6 on v5

--- a/solution.py
+++ b/solution.py
@@ -455,7 +455,7 @@
     pass_on(*z_piece(1), Z_RELAY_SENT)
 
     lag_y, lag_x, lag_m = 0, 2, 4
-    lag_o = steps + 1
+    lag_o = steps
     lag_n, lag_f, lag_c = lag_o + 2, lag_o + 4, lag_o + 6
 
     def stage(s, lag, first, last, work):
@@ -518,11 +518,11 @@
         at_step(s, lag_m + steps - 1, turn, 1)
         stage(s, lag_o, 0, steps, start_opposite)
         at_step(s, lag_o + steps, w_opposite, 0)
+        stage(s, lag_n, 0, steps, start_neighbour)
         at_step(s, lag_o + steps + 1, w_opposite, 1)
-        stage(s, lag_n, 0, steps, start_neighbour)
         at_step(s, lag_n + steps, w_neighbour, 0)
+        stage(s, lag_f, 0, steps, finish)
         at_step(s, lag_n + steps + 1, w_neighbour, 1)
-        stage(s, lag_f, 0, steps, finish)
         stage(s, lag_c + steps - plain, 0, plain, collect)
         at_step(s, lag_f + steps + 1, w_last)
         return carry

time: 134 us -> 131 us (0.978)
  Pallas kernels: 133 us -> 129 us
    pallas_call x1, Pallas kernels: 133 us -> 129 us  [shards(): pl.pallas_call(functools.partial(layer, nodes, groups), out_shape=pltpu.V...]
where the time goes in v6:
time: 131 us; the launch traced here: 130 us
  Pallas kernels  129 us (98%)
    pallas_call x1, Pallas kernels, shards(): pl.pallas_call(functools.partial(layer, nodes, groups), out_shape=pltpu.V...  129 us

profile of v6, /device:TPU:1, one launch (start us, length us, event | category | flops | bytes accessed | tf_op | source)
XLA Modules:
  0.0 130.4 jit_solution(5825211937914689282)
XLA Ops:
  0.0 129.2 %shard_map.64 = bf16[128,7168]{1,0:T(8,128)(2,1)S(1)} custom-call(bf16[128,7168]{1,0:T(8,128)(2,1)} %tok_hbm.1, s32[8,128]{1,0:T(8,128)} %bitcast.4, bf16[8,128]{1,0:T(8,128)(2,1)} %bitcast.5, bf16[2,7168,256]{2,1,0:T(8,128)(2,1)} %wg_hbm.1, bf16[2,7168,256]{2,1,0:T(8,128)(2,1)} %wu_hbm.1, bf16[512,7168]{1,0:T(8,128)(2,1)} %bitcast.3), custom_call_target="tpu_custom_call" | custom-call | tf_op jit(solution)/shard_map/pallas_call | solution.py:570
  129.2 1.2 copy.8

commit v7 on v6

--- a/solution.py
+++ b/solution.py
@@ -13,7 +13,7 @@
 LANES = 128
 CHUNK = 1024
 BATCHES = 2
-EARLY = 4
+EARLY = 2
 PACK = 16
 MESH = pl.DeviceIdType.MESH
 F32 = jnp.float32

time: 131 us -> 130 us (level)
  no operation moved by 1% of the time
where the time goes in v7:
time: 130 us
  Pallas kernels  129 us (99%)
    pallas_call x1, Pallas kernels, shards(): pl.pallas_call(functools.partial(layer, nodes, groups), out_shape=pltpu.V...  129 us

profile of v7, /device:TPU:1, one launch (start us, length us, event | category | flops | bytes accessed | tf_op | source)
XLA Modules:
  0.0 130.3 jit_solution(10825956566495897736)
XLA Ops:
  0.0 129.0 %shard_map.64 = bf16[128,7168]{1,0:T(8,128)(2,1)S(1)} custom-call(bf16[128,7168]{1,0:T(8,128)(2,1)} %tok_hbm.1, s32[8,128]{1,0:T(8,128)} %bitcast.4, bf16[8,128]{1,0:T(8,128)(2,1)} %bitcast.5, bf16[2,7168,256]{2,1,0:T(8,128)(2,1)} %wg_hbm.1, bf16[2,7168,256]{2,1,0:T(8,128)(2,1)} %wu_hbm.1, bf16[512,7168]{1,0:T(8,128)(2,1)} %bitcast.3), custom_call_target="tpu_custom_call" | custom-call | tf_op jit(solution)/shard_map/pallas_call | solution.py:570
  129.0 1.2 copy.8
